TPU v7x, 128 devices: a whole 4x4x4 slice. The times are simulated.
128 devices in a mesh: owner: 8 (over x, core), rows: 16 (over z, y).
Axes of the slice: x: 4, y: 4, z: 4, core: 2. Of those that a mesh axis runs over, the one named last changes fastest.
Arguments:
- master_gate: float32 [64, 2048, 1024], P('owner', 'rows'), may hold values from -0.1875 to 0.1875
- second_gate: bfloat16 [64, 2048, 1024], P('owner', 'rows'), may hold values from -0.0625 to 0.0625
- master_up: float32 [64, 2048, 1024], P('owner', 'rows'), may hold values from -0.1875 to 0.1875
- second_up: bfloat16 [64, 2048, 1024], P('owner', 'rows'), may hold values from -0.0625 to 0.0625
- master_down: float32 [64, 1024, 2048], P('owner', None, 'rows'), may hold values from -0.25 to 0.25
- second_down: bfloat16 [64, 1024, 2048], P('owner', None, 'rows'), may hold values from -0.09375 to 0.09375
- router_weight: float32 [2048, 64], P('rows', 'owner'), may hold values from -0.125 to 0.125
- router_gain: float32 [2048], P('rows'), may hold values from 0.25 to 1.75
Outputs:
- final_gate: bfloat16 [64, 2048, 1024], P('owner', None, 'rows')
- final_up: bfloat16 [64, 2048, 1024], P('owner', None, 'rows')
- final_down: bfloat16 [64, 1024, 2048], P('owner', 'rows')
- scale_gate: float32 [64, 1024], P('owner', 'rows')
- scale_up: float32 [64, 1024], P('owner', 'rows')
- scale_down: float32 [64, 1024], P('owner', 'rows')
- serve_router: bfloat16 [2048, 64], replicated
All inputs are finite; a program needn't handle non-finite values.
Results may differ from a plain program's by a relative error of at most 0.001.
Values may be sent and summed in bfloat16 or wider, within the bound.
No kernel may reach another device: no remote copies, remote signals or barrier semaphores. Data moves between devices by JAX's collectives and lax.ppermute only.
A program may use at most 128 MiB of HBM per device.

v0:
```python
import jax
import jax.numpy as jnp
from jax import lax
from jax.sharding import PartitionSpec as P


def sent_to_all(shard, axis):
    copies = jnp.broadcast_to(shard, (lax.axis_size(axis), *shard.shape))
    return lax.all_to_all(copies, axis, split_axis=0, concat_axis=0, tiled=True)


def taken_together(shard, axis):
    return sent_to_all(shard, axis).sum(axis=0)


def together(arrays, axis):
    ravelled, at, done = (jnp.concatenate([a.reshape(-1) for a in arrays]), 0, [])
    so_far = taken_together(ravelled, axis)
    for a in arrays:
        done.append(so_far[at : at + a.size].reshape(a.shape))
        at += a.size
    return tuple(done)


def side_by_side(arrays, axis, split_dim, concat_dim, along):
    both = jnp.concatenate(arrays, axis=along)
    result, at, done = (
        lax.all_to_all(both, axis, split_axis=split_dim, concat_axis=concat_dim, tiled=True),
        0,
        [],
    )
    for a in arrays:
        done.append(lax.slice_in_dim(result, at, at + a.shape[along], axis=along))
        at += a.shape[along]
    return tuple(done)


def split_up(shard, dim, peers):
    before, after = (shard.shape[:dim], shard.shape[dim + 1 :])
    return jnp.moveaxis(shard.reshape(*before, peers, -1, *after), dim, 0)


def piece_ends(length, count):
    unit = 8 if length >= 8 * count else 1
    return [length // unit * k // count * unit for k in range(1, count)]


def laid_out(blocks, dim):
    blocks = jnp.moveaxis(blocks, 0, dim)
    shape = blocks.shape
    return blocks.reshape(*shape[:dim], shape[dim] * shape[dim + 1], *shape[dim + 2 :])


def several_exchanges(shard, axis, pieces, split_dim, concat_dim):
    blocks = split_up(shard, split_dim, lax.axis_size(axis))
    cut = max(range(1, max(2, blocks.ndim - 1)), key=lambda d: blocks.shape[d])
    done = []
    for share in jnp.split(blocks, piece_ends(blocks.shape[cut], pieces), axis=cut):
        if share.size:
            done.append(lax.all_to_all(share, axis, split_axis=0, concat_axis=0, tiled=True))
    return laid_out(jnp.concatenate(done, axis=cut), concat_dim)


def gather_directly(shard, axis, dim):
    blocks = sent_to_all(shard, axis)
    return laid_out(blocks, dim)


def body(
    master_gate,
    second_gate,
    master_up,
    second_up,
    master_down,
    second_down,
    router_weight,
    router_gain,
):
    merged_gate = master_gate + second_gate.astype(jnp.float32)
    merged_up = master_up + second_up.astype(jnp.float32)
    merged_down = master_down + second_down.astype(jnp.float32)
    total_gate, total_up, total_down = together(
        (
            jnp.sum(merged_gate * merged_gate, axis=1),
            jnp.sum(merged_up * merged_up, axis=1),
            jnp.sum(merged_down * merged_down, axis=2),
        ),
        "rows",
    )
    scale_gate = jnp.sqrt(total_gate)
    scale_up = jnp.sqrt(total_up)
    scale_down = jnp.sqrt(total_down)
    narrow_gate, narrow_up, narrow_down = (
        (merged_gate / jnp.expand_dims(scale_gate, 1)).astype(jnp.bfloat16),
        (merged_up / jnp.expand_dims(scale_up, 1)).astype(jnp.bfloat16),
        (merged_down / jnp.expand_dims(scale_down, 2)).astype(jnp.bfloat16),
    )
    final_gate, final_up = side_by_side((narrow_gate, narrow_up), "rows", 2, 1, 0)
    final_down = several_exchanges(narrow_down, "rows", 2, 1, 2)
    scale_gate = lax.dynamic_slice_in_dim(
        scale_gate, lax.axis_index("rows") * final_gate.shape[2], final_gate.shape[2], axis=1
    )
    scale_up = lax.dynamic_slice_in_dim(
        scale_up, lax.axis_index("rows") * final_up.shape[2], final_up.shape[2], axis=1
    )
    scale_down = lax.dynamic_slice_in_dim(
        scale_down, lax.axis_index("rows") * final_down.shape[1], final_down.shape[1], axis=1
    )
    part_router = (router_weight * router_gain[:, None]).astype(jnp.bfloat16)
    row_router = gather_directly(part_router, "rows", 0)
    serve_router = gather_directly(row_router, "owner", 1)
    return (final_gate, final_up, final_down, scale_gate, scale_up, scale_down, serve_router)


def solution(mesh):
    placed = (
        P("owner", "rows", None),
        P("owner", "rows", None),
        P("owner", "rows", None),
        P("owner", "rows", None),
        P("owner", None, "rows"),
        P("owner", None, "rows"),
        P("rows", "owner"),
        P("rows"),
    )
    return jax.shard_map(
        body,
        mesh=mesh,
        in_specs=placed,
        out_specs=(
            P("owner", None, "rows"),
            P("owner", None, "rows"),
            P("owner", "rows", None),
            P("owner", "rows"),
            P("owner", "rows"),
            P("owner", "rows"),
            P(),
        ),
        check_vma=False,
    )
```

profile of v0, /device:TPU:0, one launch (start us, length us, event | category | flops | bytes accessed | tf_op | source)
XLA Modules:
  0.0 202.4 jit_solution(13047169059968651824)
XLA Ops:
  1.9 8.2 %all-to-all-start.4 = ((bf16[16,128,8]{1,2,0:T(8,128)(2,1)}), bf16[16,128,8]{1,2,0:T(8,128)(2,1)S(1)}, u32[]{:S(2)}, u32[]{:S(2)}) async-start(bf16[16,128,8]{1,2,0:T(8,128)(2,1)} %broadcast_in_dim.14), calls=%async_computation.4 | async-start | bytes 65536 | tf_op jit(solution)/shard_map/all_to_all | solution.py:9
  10.1 5.4 %copy.94 = f32[8,128,1024]{1,0,2:T(8,128)} copy(f32[8,128,1024]{2,1,0:T(8,128)} %param.10) | data formatting | bytes 8388608 | tf_op args[2]
  15.5 3.4 %copy.93 = bf16[8,128,1024]{1,0,2:T(8,128)(2,1)S(1)} copy(bf16[8,128,1024]{2,1,0:T(8,128)(2,1)} %param.11) | data formatting | bytes 4194304 | tf_op args[3]
  18.9 3.4 %multiply_reduce_fusion.1 = f32[8,1024]{0,1:T(8,128)S(1)} fusion(f32[8,128,1024]{1,0,2:T(8,128)} %copy.94, bf16[8,128,1024]{1,0,2:T(8,128)(2,1)S(1)} %copy.93), kind=kLoop, calls=%fused_computation.6 | loop fusion | flops 4186112 | bytes 6324224 | tf_op jit(solution)/shard_map/reduce_sum | solution.py:85
  22.4 5.4 %copy.91 = f32[8,128,1024]{1,0,2:T(8,128)} copy(f32[8,128,1024]{2,1,0:T(8,128)} %param.8) | data formatting | bytes 8388608 | tf_op args[0]
  27.8 4.1 %copy.90 = bf16[8,128,1024]{1,0,2:T(8,128)(2,1)} copy(bf16[8,128,1024]{2,1,0:T(8,128)(2,1)} %param.9) | data formatting | bytes 4194304 | tf_op args[1]
  32.0 4.1 %multiply_reduce_fusion.2 = f32[8,1024]{0,1:T(8,128)S(1)} fusion(f32[8,128,1024]{1,0,2:T(8,128)} %copy.91, bf16[8,128,1024]{1,0,2:T(8,128)(2,1)} %copy.90), kind=kLoop, calls=%fused_computation.8 | loop fusion | flops 4186112 | bytes 6324224 | tf_op jit(solution)/shard_map/reduce_sum | solution.py:84
  36.2 4.0 %multiply_reduce_fusion = f32[8,1024]{1,0:T(8,128)S(1)} fusion(f32[8,1024,128]{2,1,0:T(8,128)} %param.12, bf16[8,1024,128]{2,1,0:T(8,128)(2,1)} %param.13), kind=kLoop, calls=%fused_computation.4 | loop fusion | flops 4186112 | bytes 6324224 | tf_op jit(solution)/shard_map/reduce_sum | solution.py:86
  41.5 29.4 %all_to_all.41 = f32[16,1,24576]{2,1,0:T(1,128)} all-to-all(f32[16,1,24576]{2,1,0:T(1,128)S(1)} %broadcast_in_dim.6), channel_id=1, replica_groups=mesh['owner'=8,'rows'=16] {'rows'}, dimensions={0} | all-to-all | bytes 3145728 | tf_op jit(solution)/shard_map/all_to_all | solution.py:9
  71.6 4.3 %all-to-all-start.5 = ((bf16[8,2048,8]{1,2,0:T(8,128)(2,1)}), bf16[8,2048,8]{1,2,0:T(8,128)(2,1)S(1)}, u32[]{:S(2)}, u32[]{:S(2)}) async-start(bf16[8,2048,8]{1,2,0:T(8,128)(2,1)} %broadcast_in_dim.15), calls=%async_computation.5 | async-start | bytes 524288 | tf_op jit(solution)/shard_map/all_to_all | solution.py:9
  75.9 2.4 %reduce_sum.39 = f32[24576]{0:T(1024)S(1)} reduce(f32[16,1,24576]{2,1,0:T(1,128)} %all_to_all.41, f32[]{:T(128)} %constant.5.clone.1), dimensions={0,1}, to_apply=%region_3.0 | reduce | flops 368640 | bytes 1671172 | tf_op jit(solution)/shard_map/reduce_sum | solution.py:13
  78.4 3.4 %divide_convert_fusion = bf16[8,1024,128]{2,1,0:T(8,128)(2,1)S(1)} fusion(f32[8,1024,128]{2,1,0:T(8,128)} %param.12, bf16[8,1024,128]{2,1,0:T(8,128)(2,1)} %param.13, f32[8,1024]{1,0:T(8,128)S(1)} %sqrt.23), kind=kLoop, calls=%fused_computation.1 | loop fusion | flops 4194304 | bytes 8421376 | tf_op jit(solution)/shard_map/convert_element_type | solution.py:96
  84.3 3.7 %all-to-all-start.2 = ((bf16[16,8,32,128]{3,2,1,0:T(8,128)(2,1)}), bf16[16,8,32,128]{3,2,1,0:T(8,128)(2,1)S(1)}, u32[]{:S(2)}, u32[]{:S(2)}) async-start(bf16[16,8,32,128]{3,2,1,0:T(8,128)(2,1)} %copy.102), calls=%async_computation.2 | async-start | bytes 2097152 | tf_op jit(solution)/shard_map/all_to_all | solution.py:60
  89.0 2.3 %copy.103 = bf16[16,8,32,128]{3,2,1,0:T(8,128)(2,1)} copy(bf16[16,8,32,128]{3,2,0,1:T(8,128)(2,1)} %get-tuple-element.10) | data formatting | bytes 2097152 | tf_op jit(solution)/shard_map/split | solution.py:58
  91.3 16.3 %all-to-all-done.2 = bf16[16,8,32,128]{3,2,1,0:T(8,128)(2,1)S(1)} async-done(((bf16[16,8,32,128]{3,2,1,0:T(8,128)(2,1)}), bf16[16,8,32,128]{3,2,1,0:T(8,128)(2,1)S(1)}, u32[]{:S(2)}, u32[]{:S(2)}) %all-to-all-start.2) | async-done | bytes 1048608 | tf_op jit(solution)/shard_map/all_to_all | solution.py:60
  107.6 4.5 %all-to-all-start.3 = ((bf16[16,8,32,128]{3,2,1,0:T(8,128)(2,1)}), bf16[16,8,32,128]{3,2,1,0:T(8,128)(2,1)}, u32[]{:S(2)}, u32[]{:S(2)}) async-start(bf16[16,8,32,128]{3,2,1,0:T(8,128)(2,1)} %copy.103), calls=%async_computation.3 | async-start | bytes 2097152 | tf_op jit(solution)/shard_map/all_to_all | solution.py:60
  112.2 4.6 %divide_convert_fusion.2 = bf16[8,128,1024]{1,0,2:T(8,128)(2,1)} fusion(f32[8,128,1024]{1,0,2:T(8,128)} %copy.91, bf16[8,128,1024]{1,0,2:T(8,128)(2,1)} %copy.90, f32[8,1024]{0,1:T(8,128)} %copy.97), kind=kLoop, calls=%fused_computation.3 | loop fusion | flops 4194304 | bytes 8421376 | tf_op jit(solution)/shard_map/convert_element_type | solution.py:94
  117.8 4.1 %divide_convert_fusion.1 = bf16[8,128,1024]{1,0,2:T(8,128)(2,1)S(1)} fusion(f32[8,128,1024]{1,0,2:T(8,128)} %copy.94, bf16[8,128,1024]{1,0,2:T(8,128)(2,1)S(1)} %copy.93, f32[8,1024]{0,1:T(8,128)} %copy.98), kind=kLoop, calls=%fused_computation.2 | loop fusion | flops 4194304 | bytes 8421376 | tf_op jit(solution)/shard_map/convert_element_type | solution.py:95
  121.9 2.7 %pad_maximum_fusion = bf16[16,128,1024]{1,0,2:T(8,128)(2,1)} fusion(bf16[8,128,1024]{1,0,2:T(8,128)(2,1)S(1)} %divide_convert_fusion.1, bf16[8,128,1024]{1,0,2:T(8,128)(2,1)S(1)} %copy-done), kind=kLoop, calls=%fused_computation | loop fusion | flops 8388608 | bytes 8388608 | tf_op jit(solution)/shard_map/concatenate | solution.py:26
  124.6 5.2 %all-to-all-done.3 = bf16[16,8,32,128]{3,2,1,0:T(8,128)(2,1)} async-done(((bf16[16,8,32,128]{3,2,1,0:T(8,128)(2,1)}), bf16[16,8,32,128]{3,2,1,0:T(8,128)(2,1)}, u32[]{:S(2)}, u32[]{:S(2)}) %all-to-all-start.3) | async-done | bytes 1048608 | tf_op jit(solution)/shard_map/all_to_all | solution.py:60
  129.8 4.5 %all-to-all-start.1 = ((bf16[16,128,1024]{1,0,2:T(8,128)(2,1)}), bf16[16,128,1024]{1,0,2:T(8,128)(2,1)}, u32[]{:S(2)}, u32[]{:S(2)}) async-start(bf16[16,128,1024]{1,0,2:T(8,128)(2,1)} %pad_maximum_fusion), calls=%async_computation.1 | async-start | bytes 8388608 | tf_op jit(solution)/shard_map/all_to_all | solution.py:28
  136.3 2.9 %copy_bitcast_fusion = bf16[8,64,2048]{2,1,0:T(8,128)(2,1)} fusion(bf16[16,8,32,128]{3,2,1,0:T(8,128)(2,1)} %all-to-all-done.3, bf16[16,8,32,128]{3,2,1,0:T(8,128)(2,1)S(1)} %all-to-all-done.2), kind=kLoop, calls=%fused_computation.10 | loop fusion | flops 4194304 | bytes 4194304 | tf_op jit(solution)/shard_map/reshape | solution.py:51
  139.2 54.5 %all-to-all-done.1 = bf16[16,128,1024]{1,0,2:T(8,128)(2,1)} async-done(((bf16[16,128,1024]{1,0,2:T(8,128)(2,1)}), bf16[16,128,1024]{1,0,2:T(8,128)(2,1)}, u32[]{:S(2)}, u32[]{:S(2)}) %all-to-all-start.1) | async-done | bytes 4194336 | tf_op jit(solution)/shard_map/all_to_all | solution.py:28
  193.7 3.3 %copy.99 = bf16[16,128,1024]{1,2,0:T(8,128)(2,1)S(1)} copy(bf16[16,128,1024]{1,0,2:T(8,128)(2,1)} %all-to-all-done.1) | data formatting | bytes 8388608 | tf_op jit(solution)/shard_map/all_to_all | solution.py:28
  (28 shorter events, 15.6 us)
Async XLA Ops:
  1.9 38.3 %all-to-all-start.4 = ((bf16[16,128,8]{1,2,0:T(8,128)(2,1)}), bf16[16,128,8]{1,2,0:T(8,128)(2,1)S(1)}, u32[]{:S(2)}, u32[]{:S(2)}) async-start(bf16[16,128,8]{1,2,0:T(8,128)(2,1)} %broadcast_in_dim.14), calls=%async_computation.4 | async-start | bytes 65536 | tf_op jit(solution)/shard_map/all_to_all | solution.py:9
  71.6 12.7 %all-to-all-start.5 = ((bf16[8,2048,8]{1,2,0:T(8,128)(2,1)}), bf16[8,2048,8]{1,2,0:T(8,128)(2,1)S(1)}, u32[]{:S(2)}, u32[]{:S(2)}) async-start(bf16[8,2048,8]{1,2,0:T(8,128)(2,1)} %broadcast_in_dim.15), calls=%async_computation.5 | async-start | bytes 524288 | tf_op jit(solution)/shard_map/all_to_all | solution.py:9
  84.3 23.3 %all-to-all-start.2 = ((bf16[16,8,32,128]{3,2,1,0:T(8,128)(2,1)}), bf16[16,8,32,128]{3,2,1,0:T(8,128)(2,1)S(1)}, u32[]{:S(2)}, u32[]{:S(2)}) async-start(bf16[16,8,32,128]{3,2,1,0:T(8,128)(2,1)} %copy.102), calls=%async_computation.2 | async-start | bytes 2097152 | tf_op jit(solution)/shard_map/all_to_all | solution.py:60
  107.6 22.1 %all-to-all-start.3 = ((bf16[16,8,32,128]{3,2,1,0:T(8,128)(2,1)}), bf16[16,8,32,128]{3,2,1,0:T(8,128)(2,1)}, u32[]{:S(2)}, u32[]{:S(2)}) async-start(bf16[16,8,32,128]{3,2,1,0:T(8,128)(2,1)} %copy.103), calls=%async_computation.3 | async-start | bytes 2097152 | tf_op jit(solution)/shard_map/all_to_all | solution.py:60
  117.7 4.1 %copy-start = (bf16[8,128,1024]{1,0,2:T(8,128)(2,1)S(1)}, bf16[8,128,1024]{1,0,2:T(8,128)(2,1)}, u32[]{:S(2)}) copy-start(bf16[8,128,1024]{1,0,2:T(8,128)(2,1)} %divide_convert_fusion.2) | copy-start | bytes 6291460
  129.8 63.9 %all-to-all-start.1 = ((bf16[16,128,1024]{1,0,2:T(8,128)(2,1)}), bf16[16,128,1024]{1,0,2:T(8,128)(2,1)}, u32[]{:S(2)}, u32[]{:S(2)}) async-start(bf16[16,128,1024]{1,0,2:T(8,128)(2,1)} %pad_maximum_fusion), calls=%async_computation.1 | async-start | bytes 8388608 | tf_op jit(solution)/shard_map/all_to_all | solution.py:28
where the time goes:
time: 203 us; the launch traced here: 202 us
  waiting for transfers between devices  76.1 us (37%)
  local copies, waits for them, and re-layouts  38.8 us (19%)
  other arithmetic  32.3 us (16%)
  blocking collectives  29.4 us (14%)
  starting transfers between devices  25.2 us (12%)
    all_to_all x1, waiting for transfers between devices, side_by_side(): lax.all_to_all(both, axis, split_axis=split_dim, concat_axis=concat_dim,...  54.5 us
    all_to_all x1, blocking collectives, sent_to_all(): return lax.all_to_all(copies, axis, split_axis=0, concat_axis=0, tiled=True)  29.4 us
    all_to_all x2, waiting for transfers between devices, several_exchanges(): lax.all_to_all(share, axis, split_axis=0, concat_axis=0, tiled=True)  21.5 us
    unnamed x9, local copies, waits for them, and re-layouts  20 us
    all_to_all x2, starting transfers between devices, sent_to_all(): return lax.all_to_all(copies, axis, split_axis=0, concat_axis=0, tiled=True)  12.5 us
    all_to_all x2, starting transfers between devices, several_exchanges(): lax.all_to_all(share, axis, split_axis=0, concat_axis=0, tiled=True)  8.17 us
    split x3, local copies, waits for them, and re-layouts, several_exchanges(): jnp.split(blocks, piece_ends(blocks.shape[cut], pieces), axis=cut)  4.8 us
    convert_element_type x1, other arithmetic, body(): (merged_gate / jnp.expand_dims(scale_gate, 1)).astype(jnp.bfloat16)  4.56 us
  transfers between devices with their start and end apart: 5, of which 3 were waited for; matrix products, arithmetic and copies ran while one was open for 29% of the time, Pallas kernels for 0%

commit v1 on v0

v1 whole, which is shorter than its diff:
```python
import jax
import jax.numpy as jnp
import numpy as np
from jax import lax
from jax.experimental import pallas as pl
from jax.experimental.pallas import tpu as pltpu
from jax.sharding import PartitionSpec as P

F32, BF16 = jnp.float32, jnp.bfloat16
LANES = 128
MIB = 1 << 20


WAYS = (
    (2, 2), (1, 2), (2, 1), (3, 2), (2, 3), (0, 2), (2, 0),
    (1, 1), (3, 3), (1, 3), (3, 1), (0, 1), (0, 3), (1, 0), (3, 0),
)
ORDER = WAYS + ((0, 0),)
FIRST = 4
GROUPS = ((15, 0, 1, 2, 3, 4, 5, 6), (7, 8, 9, 10), (11, 12, 13, 14))


def away(row, way):
    z, y = lax.div(row, 4) + (way[0] + 4), lax.rem(row, 4) + (way[1] + 4)
    return lax.rem(z, 4) * 4 + lax.rem(y, 4)


def cost(flops, moved):
    return pl.CostEstimate(flops=flops, bytes_accessed=moved, transcendentals=0)


VMEM = pl.BlockSpec(memory_space=pltpu.VMEM)
ANY = pl.BlockSpec(memory_space=pl.ANY)


def sums_kernel(*refs):
    sources, out, held, columns, arrived = refs[:8], refs[8], refs[9:17], refs[17], refs[18]
    experts = sources[0].shape[0]
    groups = sources[4].shape[1] // LANES
    small = [
        pltpu.make_async_copy(sources[i], held[i], arrived.at[6, i - 6]) for i in (6, 7)
    ]
    for copy in small:
        copy.start()

    def fetch(i, e):
        return pltpu.make_async_copy(sources[i].at[e], held[i].at[e], arrived.at[i, e])

    for e in range(experts):
        for i in range(6):
            fetch(i, e).start()
    columns[...] = jnp.zeros_like(columns)
    for copy in small:
        copy.wait()
    out[3 * experts] = (held[6][...] * held[7][...]).astype(BF16).astype(F32)
    lane = lax.broadcasted_iota(jnp.int32, columns.shape, 1)

    def expert(e, carry):
        for i in range(6):
            fetch(i, e).wait()
        for t in range(2):
            m, s = held[2 * t], held[2 * t + 1]
            for g in range(groups):
                part = slice(g * LANES, (g + 1) * LANES)
                x = m[e, :, part] + s[e, :, part].astype(F32)
                out[t * experts + e, g : g + 1, :] = jnp.sum(x * x, axis=0, keepdims=True)
        so_far = columns[...]
        for g in range(groups):
            part = slice(g * LANES, (g + 1) * LANES)
            x = held[4][e, part] + held[5][e, part].astype(F32)
            total = jnp.sum(x * x, axis=1, keepdims=True)
            so_far = jnp.where(lane == e * groups + g, total, so_far)
        columns[...] = so_far
        return carry

    lax.fori_loop(0, experts, expert, 0)
    rows = columns[...].T
    for e in range(experts):
        out[2 * experts + e] = rows[e * groups : (e + 1) * groups]


def local_sums(mg, sg, mu, su, md, sd, w, gain):
    experts, _, width = mg.shape
    arrays = (mg, sg, mu, su, md, sd, w, gain)
    return pl.pallas_call(
        sums_kernel,
        in_specs=[ANY] * 8,
        out_specs=VMEM,
        out_shape=jax.ShapeDtypeStruct((3 * experts + 1, width // LANES, LANES), F32),
        scratch_shapes=[pltpu.VMEM(a.shape, a.dtype) for a in arrays]
        + [pltpu.VMEM((LANES, LANES), F32), pltpu.SemaphoreType.DMA((7, experts))],
        compiler_params=pltpu.CompilerParams(vmem_limit_bytes=24 * MIB),
        cost_estimate=cost(9 * mg.size, 18 * mg.size),
        name="sums",
    )(*arrays)


def turn_kernel(m, s, out):
    x = m[0] + s[0].astype(F32)
    for g in range(x.shape[1] // LANES):
        out[0, g * LANES : (g + 1) * LANES, :] = x[:, g * LANES : (g + 1) * LANES].T


def turned(m, s):
    experts, rows, width = m.shape
    tall = pl.BlockSpec((1, rows, width), lambda e: (e, 0, 0))
    return pl.pallas_call(
        turn_kernel,
        grid=(experts,),
        in_specs=[tall, tall],
        out_specs=pl.BlockSpec((1, width, rows), lambda e: (e, 0, 0)),
        out_shape=jax.ShapeDtypeStruct((experts, width, rows), F32),
        compiler_params=pltpu.CompilerParams(vmem_limit_bytes=8 * MIB),
        cost_estimate=cost(8 * m.size, 10 * m.size),
    )(m, s)


def merge_kernel(m, s, out):
    out[...] = m[...] + s[...].astype(F32)


def merged(m, s):
    flat = pl.BlockSpec((1, *m.shape[1:]), lambda e: (e, 0, 0))
    return pl.pallas_call(
        merge_kernel,
        grid=(m.shape[0],),
        in_specs=[flat, flat],
        out_specs=flat,
        out_shape=jax.ShapeDtypeStruct(m.shape, F32),
        compiler_params=pltpu.CompilerParams(vmem_limit_bytes=8 * MIB),
        cost_estimate=cost(2 * m.size, 10 * m.size),
        name="merge_down",
    )(m, s)


def fold_kernel(sums, a, b, c, d, out):
    out[:sums] = (a[:sums] + b[:sums]) + (c[:sums] + d[:sums])
    pieces = a.shape[0] - sums
    for k, part in enumerate((a, b, c, d)):
        out[sums + k * pieces : sums + (k + 1) * pieces] = part[sums:]


def folded(sums, parts):
    pieces = parts[0].shape[0] - sums
    out = jax.ShapeDtypeStruct((sums + 4 * pieces, *parts[0].shape[1:]), F32)
    return pl.pallas_call(
        lambda *refs: fold_kernel(sums, *refs),
        out_shape=out,
        compiler_params=pltpu.CompilerParams(vmem_limit_bytes=4 * MIB),
        cost_estimate=cost(out.size, 24 * out.size),
    )(*parts)


def in_three(x):
    high = x.astype(BF16).astype(F32)
    middle = (x - high).astype(BF16).astype(F32)
    return [high, middle, (x - high - middle).astype(BF16).astype(F32)]


def picker(combos):
    c = np.arange(LANES)[:, None]
    n = np.arange(combos * LANES)[None, :]
    return jnp.asarray((c % combos == n // LANES) & (c < 3 * combos), BF16)


def divide(first, pick, scales, sources, outs):
    experts, _, lanes = sources[0].shape
    for k, out in enumerate(outs):
        to = away(lax.axis_index("rows"), ORDER[first + k])
        rows = pl.ds(pl.multiple_of(to * out.shape[2], out.shape[2]), out.shape[2])
        for t, source in enumerate(sources):
            combos = slice(t * experts * lanes, (t + 1) * experts * lanes)
            scale = jnp.dot(scales[rows, :], pick[:, combos], preferred_element_type=F32)
            for e in range(experts):
                part = slice(e * lanes, (e + 1) * lanes)
                out[t, e] = (source[e, rows, :] / scale[:, part]).astype(BF16)


def first_kernel(pick, a, b, c, d, tg, tu, td, scale, kept, scales, *outs):
    sums, groups, _ = scale.shape
    root = jnp.sqrt((a[:sums] + b[:sums]) + (c[:sums] + d[:sums]))
    scale[...] = root
    pieces = a.shape[0] - sums
    for k, part in enumerate((a, b, c, d)):
        kept[k * pieces : (k + 1) * pieces] = part[sums:]
    rest = jnp.zeros((LANES - 3 * sums, LANES), F32)
    for g in range(groups):
        block = jnp.concatenate(in_three(root[:, g, :]) + [rest], axis=0)
        scales[g * LANES : (g + 1) * LANES] = block.T.astype(BF16)
    divide(0, pick, scales, (tg, tu, td), outs)


def rest_kernel(first, pick, scales, tg, tu, td, *outs):
    divide(first, pick, scales, (tg, tu, td), outs)


def scaled(pick, parts, tg, tu, td, ends):
    experts, width, rows = tg.shape
    peers = len(ORDER)
    sums = 3 * experts
    piece = pltpu.VMEM((3, experts, width // peers, rows), BF16)
    size = 3 * experts * (width // peers) * rows
    outs = [
        jax.ShapeDtypeStruct((sums, *parts[0].shape[1:]), F32),
        jax.ShapeDtypeStruct((4 * (parts[0].shape[0] - sums), *parts[0].shape[1:]), F32),
        pltpu.VMEM((width, LANES), BF16),
    ]
    moved = lambda count: 6 * count * size
    scale, kept, scales, *pieces = pl.pallas_call(
        first_kernel,
        in_specs=[VMEM] * 8,
        out_specs=[VMEM] * (3 + ends[0]),
        out_shape=outs + [piece] * ends[0],
        compiler_params=pltpu.CompilerParams(vmem_limit_bytes=8 * MIB),
        cost_estimate=cost(6 * size * ends[0], moved(ends[0])),
        name="scale_0",
    )(pick, *parts, tg, tu, td)
    for first, end in zip(ends, ends[1:]):
        pieces += pl.pallas_call(
            lambda *refs, first=first: rest_kernel(first, *refs),
            in_specs=[VMEM] * 5,
            out_specs=[VMEM] * (end - first),
            out_shape=[piece] * (end - first),
            compiler_params=pltpu.CompilerParams(vmem_limit_bytes=8 * MIB),
            cost_estimate=cost(6 * size * (end - first), moved(end - first)),
        )(pick, scales, tg, tu, td)
    return scale, kept, pieces


def place_kernel(ways, *refs):
    count = len(ways)
    pieces, outs, done = refs[:count], refs[-4:-1], refs[-1]
    copies = []
    for k, piece in enumerate(pieces):
        back = [-step for step in ways[k]]
        came_from = away(lax.axis_index("rows"), back)
        columns = pl.ds(pl.multiple_of(came_from * LANES, LANES), LANES)
        for t, out in enumerate(outs):
            copies.append(pltpu.make_async_copy(piece.at[t], out.at[:, :, columns], done.at[k, t]))
    for copy in copies:
        copy.start()
    for copy in copies:
        copy.wait()


def side_by_side(pieces, groups):
    _, experts, rows, lanes = pieces[0].shape
    out = pltpu.HBM((experts, rows, len(ORDER) * lanes), BF16)
    so_far = ()
    for group in groups:
        count = len(group)
        ways = [ORDER[k] for k in group]
        so_far = pl.pallas_call(
            lambda *refs, ways=ways: place_kernel(ways, *refs),
            in_specs=[VMEM] * count + [ANY] * len(so_far),
            out_specs=[ANY] * 3,
            out_shape=[out] * 3,
            scratch_shapes=[pltpu.SemaphoreType.DMA((count, 3))],
            input_output_aliases={count + t: t for t in range(len(so_far))},
            compiler_params=pltpu.CompilerParams(vmem_limit_bytes=8 * MIB),
            cost_estimate=cost(0, 4 * count * pieces[0].size),
        )(*[pieces[k] for k in group], *so_far)
    return so_far


def order_rows_kernel(pieces, out):
    for a in range(4):
        for b in range(4):
            place = away(lax.axis_index("rows"), (-a, -b))
            out[:, pl.ds(pl.multiple_of(place * LANES, LANES), LANES)] = pieces[4 * a + b].astype(BF16)


def stack_kernel(a, b, c, d, out):
    for k, part in enumerate((a, b, c, d)):
        out[k] = part[...]


def own_scales_kernel(scale, *outs):
    row = lax.axis_index("rows")
    experts, width = outs[0].shape
    group, half = lax.div(row * width, LANES), lax.rem(row * width, LANES)
    for t, out in enumerate(outs):
        x = scale[t * experts : (t + 1) * experts, group, :]
        out[...] = jnp.where(half > 0, pltpu.roll(x, LANES - width, 1), x)[:, :width]


def own_scales(scale, experts):
    out = jax.ShapeDtypeStruct((experts, 64), F32)
    return pl.pallas_call(
        own_scales_kernel,
        in_specs=[VMEM],
        out_specs=[VMEM] * 3,
        out_shape=[out] * 3,
        compiler_params=pltpu.CompilerParams(vmem_limit_bytes=4 * MIB),
        cost_estimate=cost(0, 4 * scale.size),
        name="own_scales",
    )(scale)


def order_owners_kernel(a, b, c, d, other, out):
    own = lax.axis_index("owner")
    x, core = lax.div(own, 2), lax.rem(own, 2)
    for k in range(4):
        place = lax.rem(x + 4 - k, 4) * 2
        out[pl.ds(pl.multiple_of((place + core) * 8, 8), 8), :] = (a, b, c, d)[k][...]
        out[pl.ds(pl.multiple_of((place + 1 - core) * 8, 8), 8), :] = other[k]


def placed_by(kernel, arrays, shape):
    return pl.pallas_call(
        kernel,
        in_specs=[VMEM] * len(arrays),
        out_specs=VMEM,
        out_shape=jax.ShapeDtypeStruct(shape, BF16),
        compiler_params=pltpu.CompilerParams(vmem_limit_bytes=4 * MIB),
        cost_estimate=cost(0, 1 << 18),
    )(*arrays)


def in_hbm(a):
    return pltpu.with_memory_space_constraint(a, pltpu.HBM)


def pairs(way):
    return [(i, (i // 4 + way[0]) % 4 * 4 + (i % 4 + way[1]) % 4) for i in range(16)]


ALONG_Y = [pairs((0, k)) for k in (1, 2, 3)]
ALONG_Z = [pairs((k, 0)) for k in (1, 2, 3)]
ALONG_X = [[(i, (i // 2 + k) % 4 * 2 + i % 2) for i in range(8)] for k in (1, 2, 3)]
OTHER_CORE = [(i, i ^ 1) for i in range(8)]


def from_all(a, axis, ways):
    came = [a]
    for way in ways:
        came.append(lax.ppermute(a, axis, way))
    return came


def body(mg, sg, mu, su, md, sd, w, gain):
    experts = mg.shape[0]
    sums = 3 * experts
    here = local_sums(*[in_hbm(a) for a in (mg, sg, mu, su, md, sd, w.T, gain[None, :])])
    near = from_all(here, "rows", ALONG_Y)
    line = folded(sums, near)
    far = from_all(line, "rows", ALONG_Z)
    tg = turned(mg, sg)
    tu = turned(mu, su)
    td = merged(md, sd)
    scale, pieces, send = scaled(picker(sums), far, tg, tu, td, (FIRST, 16))
    came = []
    for k, way in enumerate(WAYS):
        came.append(lax.ppermute(send[k], "rows", pairs(way)))
    came.append(send[-1])
    columns = placed_by(order_rows_kernel, (pieces,), (8, 16 * LANES))
    columns = from_all(columns, "owner", ALONG_X)
    other = lax.ppermute(placed_by(stack_kernel, columns, (4, 8, 16 * LANES)), "owner", OTHER_CORE)
    router = placed_by(order_owners_kernel, (*columns, other), (64, 16 * LANES)).T
    mine = own_scales(scale, experts)
    g, u, d = side_by_side(came, GROUPS)
    return (jnp.swapaxes(g, 1, 2), jnp.swapaxes(u, 1, 2), d, mine[0], mine[1], mine[2], router)


def solution(mesh):
    placed = (
        P("owner", "rows", None),
        P("owner", "rows", None),
        P("owner", "rows", None),
        P("owner", "rows", None),
        P("owner", None, "rows"),
        P("owner", None, "rows"),
        P("rows", "owner"),
        P("rows"),
    )
    return jax.shard_map(
        body,
        mesh=mesh,
        in_specs=placed,
        out_specs=(
            P("owner", None, "rows"),
            P("owner", None, "rows"),
            P("owner", "rows", None),
            P("owner", "rows"),
            P("owner", "rows"),
            P("owner", "rows"),
            P(),
        ),
        check_vma=False,
    )
```

time: 203 us -> 144 us (0.71)
  local copies, waits for them, and re-layouts: 38.8 us -> 2.97 us
  other arithmetic: 32.3 us -> 0 us
  blocking collectives: 29.4 us -> 0 us
  starting transfers between devices: 25.2 us -> 46.6 us
  Pallas kernels: 0 us -> 19.3 us
  waiting for transfers between devices: 76.1 us -> 72.7 us
    all_to_all x5 -> x0, waiting for transfers between devices: 76.1 us -> none  [the longest x1 54.5 us: side_by_side(): lax.all_to_all(both, axis, split_axis=split_dim, concat_axis=concat_dim,...]
    ppermute x0 -> x25, waiting for transfers between devices: none -> 72.7 us  [the longest x15 61.9 us: body(): came.append(lax.ppermute(send[k], 'rows', pairs(way)))]
    ppermute x0 -> x25, starting transfers between devices: none -> 46.6 us  [the longest x15 31.9 us: body(): came.append(lax.ppermute(send[k], 'rows', pairs(way)))]
    all_to_all x1 -> x0, blocking collectives: 29.4 us -> none  [sent_to_all(): return lax.all_to_all(copies, axis, split_axis=0, concat_axis=0, tiled=True)]
    all_to_all x5 -> x0, starting transfers between devices: 25.2 us -> none  [the longest x2 12.5 us: sent_to_all(): return lax.all_to_all(copies, axis, split_axis=0, concat_axis=0, tiled=True)]
    pallas_call x0 -> x14, Pallas kernels: none -> 19.3 us  [the longest x1 7.45 us: local_sums(): pl.pallas_call(sums_kernel, in_specs=[ANY] * 8, out_specs=VMEM, out_shape...]
    unnamed x9 -> x14, local copies, waits for them, and re-layouts: 20 us -> 2.97 us
    reduce_sum x4 -> x0, other arithmetic: 13.9 us -> none  [the longest x1 4.05 us: body(): jnp.sum(merged_gate * merged_gate, axis=1)]
  transfers between devices with their start and end apart: 5 -> 25, of which waited for: 3 -> 10; matrix products, arithmetic and copies ran while one was open for 29% -> 0% of each run, Pallas kernels for 0% -> 7%
where the time goes in v1:
time: 144 us; the launch traced here: 142 us
  waiting for transfers between devices  72.7 us (50%)
  starting transfers between devices  46.6 us (32%)
  Pallas kernels  19.3 us (13%)
  local copies, waits for them, and re-layouts  2.97 us (2%)
    ppermute x15, waiting for transfers between devices, body(): came.append(lax.ppermute(send[k], 'rows', pairs(way)))  61.9 us
    ppermute x15, starting transfers between devices, body(): came.append(lax.ppermute(send[k], 'rows', pairs(way)))  31.9 us
    ppermute x9, starting transfers between devices, from_all(): came.append(lax.ppermute(a, axis, way))  14.7 us
    ppermute x9, waiting for transfers between devices, from_all(): came.append(lax.ppermute(a, axis, way))  10.8 us
    pallas_call x1, Pallas kernels, local_sums(): pl.pallas_call(sums_kernel, in_specs=[ANY] * 8, out_specs=VMEM, out_shape...  7.45 us
    pallas_call x3, Pallas kernels, side_by_side(): pl.pallas_call(lambda *refs, ways=ways: place_kernel(ways, *refs), in_spe...  4.33 us
    pallas_call x2, Pallas kernels, turned(): pl.pallas_call(turn_kernel, grid=(experts,), in_specs=[tall, tall], out_s...  3.27 us
    unnamed x14, local copies, waits for them, and re-layouts  2.97 us
  transfers between devices with their start and end apart: 25, of which 10 were waited for; matrix products, arithmetic and copies ran while one was open for 0% of the time, Pallas kernels for 7%

profile of v1, /device:TPU:0, one launch (start us, length us, event | category | flops | bytes accessed | tf_op | source)
XLA Modules:
  0.0 142.4 jit_solution(16468069244116228520)
XLA Ops:
  0.7 7.4 %sums.1.refs_0_ = f32[25,8,128]{2,1,0:T(8,128)S(1)} custom-call(f32[8,128,1024]{2,1,0:T(8,128)} %m.3, bf16[8,128,1024]{2,1,0:T(8,128)(2,1)} %s.3, f32[8,128,1024]{2,1,0:T(8,128)} %m.4, bf16[8,128,1024]{2,1,0:T(8,128)(2,1)} %s.4, f32[8,1024,128]{2,1,0:T(8,128)} %m.5, bf16[8,1024,128]{2,1,0:T(8,128)(2,1)} %s.5, f32[8,128]{1,0:T(8,128)} %bitcast.8, ...), custom_call_target="tpu_custom_call" | custom-call | flops 9437184 | bytes 18874368 | tf_op jit(solution)/shard_map/sums/pallas_call | solution.py:85
  8.1 3.2 %collective-permute-start.2 = (f32[25,8,128]{2,1,0:T(8,128)S(1)}, f32[25,8,128]{2,1,0:T(8,128)S(1)}, u32[]{:S(2)}, u32[]{:S(2)}) collective-permute-start(f32[25,8,128]{2,1,0:T(8,128)S(1)} %sums.1.refs_0_), channel_id=1, source_target_pairs={{0,3},{1,0},{2,1},{3,2},{4,7},{5,4},{6,5},{7,6},{8,11},{9,8},{10,9... | collective-permute-start | bytes 307208 | tf_op jit(solution)/shard_map/ppermute | solution.py:337
  12.9 2.8 %collective-permute-done.2.refs_3_ = f32[25,8,128]{2,1,0:T(8,128)S(1)} collective-permute-done((f32[25,8,128]{2,1,0:T(8,128)S(1)}, f32[25,8,128]{2,1,0:T(8,128)S(1)}, u32[]{:S(2)}, u32[]{:S(2)}) %collective-permute-start.2) | collective-permute-done | bytes 102432 | tf_op jit(solution)/shard_map/ppermute | solution.py:337
  15.7 2.6 %collective-permute-done.1.refs_2_ = f32[25,8,128]{2,1,0:T(8,128)S(1)} collective-permute-done((f32[25,8,128]{2,1,0:T(8,128)S(1)}, f32[25,8,128]{2,1,0:T(8,128)S(1)}, u32[]{:S(2)}, u32[]{:S(2)}) %collective-permute-start.1) | collective-permute-done | bytes 102432 | tf_op jit(solution)/shard_map/ppermute | solution.py:337
  19.4 4.1 %collective-permute-start.5 = (f32[28,8,128]{2,1,0:T(8,128)S(1)}, f32[28,8,128]{2,1,0:T(8,128)S(1)}, u32[]{:S(2)}, u32[]{:S(2)}) collective-permute-start(f32[28,8,128]{2,1,0:T(8,128)S(1)} %shard_map.144.a), channel_id=1, source_target_pairs={{0,12},{1,13},{2,14},{3,15},{4,0},{5,1},{6,2},{7,3},{8,4},{9,5},{1... | collective-permute-start | bytes 344072 | tf_op jit(solution)/shard_map/ppermute | solution.py:337
  23.5 1.3 collective-permute-start.3
  25.2 1.7 %copy-done.1 = f32[8,128,1024]{2,1,0:T(8,128)S(1)} copy-done((f32[8,128,1024]{2,1,0:T(8,128)S(1)}, f32[8,128,1024]{2,1,0:T(8,128)}, u32[]{:S(2)}) %copy-start.1) | copy-done | bytes 4194328
  27.0 1.6 %shard_map.145.tg.refs_2_ = f32[8,1024,128]{2,1,0:T(8,128)S(1)} custom-call(f32[8,128,1024]{2,1,0:T(8,128)S(1)} %copy-done.1, bf16[8,128,1024]{2,1,0:T(8,128)(2,1)S(1)} %copy-done.4), custom_call_target="tpu_custom_call" | custom-call | flops 8388608 | bytes 10485760 | tf_op jit(solution)/shard_map/pallas_call | solution.py:107
  29.8 1.6 %shard_map.146.tu.refs_3_ = f32[8,1024,128]{2,1,0:T(8,128)S(1)} custom-call(f32[8,128,1024]{2,1,0:T(8,128)S(1)} %copy-done.2, bf16[8,128,1024]{2,1,0:T(8,128)(2,1)S(1)} %copy-done.5), custom_call_target="tpu_custom_call" | custom-call | flops 8388608 | bytes 10485760 | tf_op jit(solution)/shard_map/pallas_call | solution.py:107
  32.6 2.8 %collective-permute-start.23 = (bf16[8,2048]{1,0:T(8,128)(2,1)S(1)}, bf16[8,2048]{1,0:T(8,128)(2,1)S(1)}, u32[]{:S(2)}, u32[]{:S(2)}) collective-permute-start(bf16[8,2048]{1,0:T(8,128)(2,1)S(1)} %shard_map.151.a), channel_id=1, source_target_pairs={{0,96},{16,112},{32,0},{48,16},{64,32},{80,48},{96,64},{112,80},{1... | collective-permute-start | bytes 98312 | tf_op jit(solution)/shard_map/ppermute | solution.py:337
  37.1 3.7 %collective-permute-done.22.c = bf16[8,2048]{1,0:T(8,128)(2,1)S(1)} collective-permute-done((bf16[8,2048]{1,0:T(8,128)(2,1)S(1)}, bf16[8,2048]{1,0:T(8,128)(2,1)S(1)}, u32[]{:S(2)}, u32[]{:S(2)}) %collective-permute-start.22) | collective-permute-done | bytes 32800 | tf_op jit(solution)/shard_map/ppermute | solution.py:337
  41.4 1.4 shard_map.147
  43.6 4.6 %collective-permute-start.11 = (bf16[3,8,64,128]{3,2,1,0:T(8,128)(2,1)S(1)}, bf16[3,8,64,128]{3,2,1,0:T(8,128)(2,1)S(1)}, u32[]{:S(2)}, u32[]{:S(2)}) collective-permute-start(bf16[3,8,64,128]{3,2,1,0:T(8,128)(2,1)S(1)} %get-tuple-element.44), channel_id=1, source_target_pairs={{0,15},{1,12},{2,13},{3,14},{4,3},{5,0},{6,1},{7,2},{8,7},{9,4},{1... | collective-permute-start | bytes 1179656 | tf_op jit(solution)/shard_map/ppermute | solution.py:354
  49.3 4.1 %collective-permute-start.19 = (bf16[3,8,64,128]{3,2,1,0:T(8,128)(2,1)S(1)}, bf16[3,8,64,128]{3,2,1,0:T(8,128)(2,1)S(1)}, u32[]{:S(2)}, u32[]{:S(2)}) collective-permute-start(bf16[3,8,64,128]{3,2,1,0:T(8,128)(2,1)S(1)} %get-tuple-element.53), channel_id=1, source_target_pairs={{0,2},{1,3},{2,0},{3,1},{4,6},{5,7},{6,4},{7,5},{8,10},{9,11},{10,... | collective-permute-start | bytes 1179656 | tf_op jit(solution)/shard_map/ppermute | solution.py:354
  53.4 13.1 %collective-permute-done.10.refs_0_ = bf16[3,8,64,128]{3,2,1,0:T(8,128)(2,1)S(1)} collective-permute-done((bf16[3,8,64,128]{3,2,1,0:T(8,128)(2,1)S(1)}, bf16[3,8,64,128]{3,2,1,0:T(8,128)(2,1)S(1)}, u32[]{:S(2)}, u32[]{:S(2)}) %collective-permute-start.10) | collective-permute-done | bytes 393248 | tf_op jit(solution)/shard_map/ppermute | solution.py:354
  67.7 6.4 %collective-permute-start.15 = (bf16[3,8,64,128]{3,2,1,0:T(8,128)(2,1)S(1)}, bf16[3,8,64,128]{3,2,1,0:T(8,128)(2,1)S(1)}, u32[]{:S(2)}, u32[]{:S(2)}) collective-permute-start(bf16[3,8,64,128]{3,2,1,0:T(8,128)(2,1)S(1)} %get-tuple-element.49), channel_id=1, source_target_pairs={{0,6},{1,7},{2,4},{3,5},{4,10},{5,11},{6,8},{7,9},{8,14},{9,15},{1... | collective-permute-start | bytes 1179656 | tf_op jit(solution)/shard_map/ppermute | solution.py:354
  74.1 35.5 %collective-permute-done.18.refs_5_ = bf16[3,8,64,128]{3,2,1,0:T(8,128)(2,1)S(1)} collective-permute-done((bf16[3,8,64,128]{3,2,1,0:T(8,128)(2,1)S(1)}, bf16[3,8,64,128]{3,2,1,0:T(8,128)(2,1)S(1)}, u32[]{:S(2)}, u32[]{:S(2)}) %collective-permute-start.18) | collective-permute-done | bytes 393248 | tf_op jit(solution)/shard_map/ppermute | solution.py:354
  109.8 7.2 %collective-permute-start.13 = (bf16[3,8,64,128]{3,2,1,0:T(8,128)(2,1)S(1)}, bf16[3,8,64,128]{3,2,1,0:T(8,128)(2,1)S(1)}, u32[]{:S(2)}, u32[]{:S(2)}) collective-permute-start(bf16[3,8,64,128]{3,2,1,0:T(8,128)(2,1)S(1)} %get-tuple-element.46), channel_id=1, source_target_pairs={{0,13},{1,14},{2,15},{3,12},{4,1},{5,2},{6,3},{7,0},{8,5},{9,6},{1... | collective-permute-start | bytes 1179656 | tf_op jit(solution)/shard_map/ppermute | solution.py:354
  117.0 3.2 %collective-permute-start.7 = (bf16[3,8,64,128]{3,2,1,0:T(8,128)(2,1)S(1)}, bf16[3,8,64,128]{3,2,1,0:T(8,128)(2,1)S(1)}, u32[]{:S(2)}, u32[]{:S(2)}) collective-permute-start(bf16[3,8,64,128]{3,2,1,0:T(8,128)(2,1)S(1)} %get-tuple-element.40), channel_id=1, source_target_pairs={{0,3},{1,0},{2,1},{3,2},{4,7},{5,4},{6,5},{7,6},{8,11},{9,8},{10,9... | collective-permute-start | bytes 1179656 | tf_op jit(solution)/shard_map/ppermute | solution.py:354
  120.2 12.0 %collective-permute-done.16.refs_3_ = bf16[3,8,64,128]{3,2,1,0:T(8,128)(2,1)S(1)} collective-permute-done((bf16[3,8,64,128]{3,2,1,0:T(8,128)(2,1)S(1)}, bf16[3,8,64,128]{3,2,1,0:T(8,128)(2,1)S(1)}, u32[]{:S(2)}, u32[]{:S(2)}) %collective-permute-start.16) | collective-permute-done | bytes 393248 | tf_op jit(solution)/shard_map/ppermute | solution.py:354
  132.2 3.2 %collective-permute-start.9 = (bf16[3,8,64,128]{3,2,1,0:T(8,128)(2,1)S(1)}, bf16[3,8,64,128]{3,2,1,0:T(8,128)(2,1)S(1)}, u32[]{:S(2)}, u32[]{:S(2)}) collective-permute-start(bf16[3,8,64,128]{3,2,1,0:T(8,128)(2,1)S(1)} %get-tuple-element.42), channel_id=1, source_target_pairs={{0,12},{1,13},{2,14},{3,15},{4,0},{5,1},{6,2},{7,3},{8,4},{9,5},{1... | collective-permute-start | bytes 1179656 | tf_op jit(solution)/shard_map/ppermute | solution.py:354
  136.9 1.8 %shard_map.148 = (bf16[8,64,2048]{2,1,0:T(8,128)(2,1)}, bf16[8,64,2048]{2,1,0:T(8,128)(2,1)}, bf16[8,64,2048]{2,1,0:T(8,128)(2,1)}) custom-call(bf16[3,8,64,128]{3,2,1,0:T(8,128)(2,1)S(1)} %get-tuple-element.47.refs_0_, bf16[3,8,64,128]{3,2,1,0:T(8,128)(2,1)S(1)} %collective-permute-done.14.refs_1_, ...), custom_call_target="tpu_custom_call" | custom-call | bytes 6291456 | tf_op jit(solution)/shard_map/pallas_call | solution.py:253
  138.7 1.3 shard_map.149
  141.2 1.2 shard_map.150
  (54 shorter events, 13.5 us)
Async XLA Ops:
  8.1 7.6 %collective-permute-start.2 = (f32[25,8,128]{2,1,0:T(8,128)S(1)}, f32[25,8,128]{2,1,0:T(8,128)S(1)}, u32[]{:S(2)}, u32[]{:S(2)}) collective-permute-start(f32[25,8,128]{2,1,0:T(8,128)S(1)} %sums.1.refs_0_), channel_id=1, source_target_pairs={{0,3},{1,0},{2,1},{3,2},{4,7},{5,4},{6,5},{7,6},{8,11},{9,8},{10,9... | collective-permute-start | bytes 307208 | tf_op jit(solution)/shard_map/ppermute | solution.py:337
  11.3 6.9 %collective-permute-start.1 = (f32[25,8,128]{2,1,0:T(8,128)S(1)}, f32[25,8,128]{2,1,0:T(8,128)S(1)}, u32[]{:S(2)}, u32[]{:S(2)}) collective-permute-start(f32[25,8,128]{2,1,0:T(8,128)S(1)} %sums.1.refs_0_), channel_id=1, source_target_pairs={{0,2},{1,3},{2,0},{3,1},{4,6},{5,7},{6,4},{7,5},{8,10},{9,11},{10,... | collective-permute-start | bytes 307208 | tf_op jit(solution)/shard_map/ppermute | solution.py:337
  11.9 7.4 %collective-permute-start = (f32[25,8,128]{2,1,0:T(8,128)S(1)}, f32[25,8,128]{2,1,0:T(8,128)S(1)}, u32[]{:S(2)}, u32[]{:S(2)}) collective-permute-start(f32[25,8,128]{2,1,0:T(8,128)S(1)} %sums.1.refs_0_), channel_id=1, source_target_pairs={{0,1},{1,2},{2,3},{3,0},{4,5},{5,6},{6,7},{7,4},{8,9},{9,10},{10,1... | collective-permute-start | bytes 307208 | tf_op jit(solution)/shard_map/ppermute | solution.py:337
  19.4 12.1 %collective-permute-start.5 = (f32[28,8,128]{2,1,0:T(8,128)S(1)}, f32[28,8,128]{2,1,0:T(8,128)S(1)}, u32[]{:S(2)}, u32[]{:S(2)}) collective-permute-start(f32[28,8,128]{2,1,0:T(8,128)S(1)} %shard_map.144.a), channel_id=1, source_target_pairs={{0,12},{1,13},{2,14},{3,15},{4,0},{5,1},{6,2},{7,3},{8,4},{9,5},{1... | collective-permute-start | bytes 344072 | tf_op jit(solution)/shard_map/ppermute | solution.py:337
  23.5 8.0 %collective-permute-start.4 = (f32[28,8,128]{2,1,0:T(8,128)S(1)}, f32[28,8,128]{2,1,0:T(8,128)S(1)}, u32[]{:S(2)}, u32[]{:S(2)}) collective-permute-start(f32[28,8,128]{2,1,0:T(8,128)S(1)} %shard_map.144.a), channel_id=1, source_target_pairs={{0,8},{1,9},{2,10},{3,11},{4,12},{5,13},{6,14},{7,15},{8,0},{9,1},... | collective-permute-start | bytes 344072 | tf_op jit(solution)/shard_map/ppermute | solution.py:337
  23.5 8.1 %collective-permute-start.3 = (f32[28,8,128]{2,1,0:T(8,128)S(1)}, f32[28,8,128]{2,1,0:T(8,128)S(1)}, u32[]{:S(2)}, u32[]{:S(2)}) collective-permute-start(f32[28,8,128]{2,1,0:T(8,128)S(1)} %shard_map.144.a), channel_id=1, source_target_pairs={{0,4},{1,5},{2,6},{3,7},{4,8},{5,9},{6,10},{7,11},{8,12},{9,13},{1... | collective-permute-start | bytes 344072 | tf_op jit(solution)/shard_map/ppermute | solution.py:337
  35.4 5.4 %collective-permute-start.22 = (bf16[8,2048]{1,0:T(8,128)(2,1)S(1)}, bf16[8,2048]{1,0:T(8,128)(2,1)S(1)}, u32[]{:S(2)}, u32[]{:S(2)}) collective-permute-start(bf16[8,2048]{1,0:T(8,128)(2,1)S(1)} %shard_map.151.a), channel_id=1, source_target_pairs={{0,64},{16,80},{32,96},{48,112},{64,0},{80,16},{96,32},{112,48},{1... | collective-permute-start | bytes 98312 | tf_op jit(solution)/shard_map/ppermute | solution.py:337
  36.2 5.1 %collective-permute-start.21 = (bf16[8,2048]{1,0:T(8,128)(2,1)S(1)}, bf16[8,2048]{1,0:T(8,128)(2,1)S(1)}, u32[]{:S(2)}, u32[]{:S(2)}) collective-permute-start(bf16[8,2048]{1,0:T(8,128)(2,1)S(1)} %shard_map.151.a), channel_id=1, source_target_pairs={{0,32},{16,48},{32,64},{48,80},{64,96},{80,112},{96,0},{112,16},{1... | collective-permute-start | bytes 98312 | tf_op jit(solution)/shard_map/ppermute | solution.py:337
  41.3 8.0 %collective-permute-start.24 = (bf16[4,8,2048]{2,1,0:T(8,128)(2,1)S(1)}, bf16[4,8,2048]{2,1,0:T(8,128)(2,1)S(1)}, u32[]{:S(2)}, u32[]{:S(2)}) collective-permute-start(bf16[4,8,2048]{2,1,0:T(8,128)(2,1)S(1)} %shard_map.152), channel_id=1, source_target_pairs={{0,16},{16,0},{32,48},{48,32},{64,80},{80,64},{96,112},{112,96},{1... | collective-permute-start | bytes 393224 | tf_op jit(solution)/shard_map/ppermute | solution.py:358
  42.8 23.7 %collective-permute-start.10 = (bf16[3,8,64,128]{3,2,1,0:T(8,128)(2,1)S(1)}, bf16[3,8,64,128]{3,2,1,0:T(8,128)(2,1)S(1)}, u32[]{:S(2)}, u32[]{:S(2)}) collective-permute-start(bf16[3,8,64,128]{3,2,1,0:T(8,128)(2,1)S(1)} %get-tuple-element.43), channel_id=1, source_target_pairs={{0,5},{1,6},{2,7},{3,4},{4,9},{5,10},{6,11},{7,8},{8,13},{9,14},{1... | collective-permute-start | bytes 1179656 | tf_op jit(solution)/shard_map/ppermute | solution.py:354
  43.6 24.1 %collective-permute-start.11 = (bf16[3,8,64,128]{3,2,1,0:T(8,128)(2,1)S(1)}, bf16[3,8,64,128]{3,2,1,0:T(8,128)(2,1)S(1)}, u32[]{:S(2)}, u32[]{:S(2)}) collective-permute-start(bf16[3,8,64,128]{3,2,1,0:T(8,128)(2,1)S(1)} %get-tuple-element.44), channel_id=1, source_target_pairs={{0,15},{1,12},{2,13},{3,14},{4,3},{5,0},{6,1},{7,2},{8,7},{9,4},{1... | collective-permute-start | bytes 1179656 | tf_op jit(solution)/shard_map/ppermute | solution.py:354
  48.2 19.5 %collective-permute-start.12 = (bf16[3,8,64,128]{3,2,1,0:T(8,128)(2,1)S(1)}, bf16[3,8,64,128]{3,2,1,0:T(8,128)(2,1)S(1)}, u32[]{:S(2)}, u32[]{:S(2)}) collective-permute-start(bf16[3,8,64,128]{3,2,1,0:T(8,128)(2,1)S(1)} %get-tuple-element.45), channel_id=1, source_target_pairs={{0,7},{1,4},{2,5},{3,6},{4,11},{5,8},{6,9},{7,10},{8,15},{9,12},{1... | collective-permute-start | bytes 1179656 | tf_op jit(solution)/shard_map/ppermute | solution.py:354
  48.2 61.4 %collective-permute-start.18 = (bf16[3,8,64,128]{3,2,1,0:T(8,128)(2,1)S(1)}, bf16[3,8,64,128]{3,2,1,0:T(8,128)(2,1)S(1)}, u32[]{:S(2)}, u32[]{:S(2)}) collective-permute-start(bf16[3,8,64,128]{3,2,1,0:T(8,128)(2,1)S(1)} %get-tuple-element.52), channel_id=1, source_target_pairs={{0,11},{1,8},{2,9},{3,10},{4,15},{5,12},{6,13},{7,14},{8,3},{9,0},... | collective-permute-start | bytes 1179656 | tf_op jit(solution)/shard_map/ppermute | solution.py:354
  49.3 60.4 %collective-permute-start.19 = (bf16[3,8,64,128]{3,2,1,0:T(8,128)(2,1)S(1)}, bf16[3,8,64,128]{3,2,1,0:T(8,128)(2,1)S(1)}, u32[]{:S(2)}, u32[]{:S(2)}) collective-permute-start(bf16[3,8,64,128]{3,2,1,0:T(8,128)(2,1)S(1)} %get-tuple-element.53), channel_id=1, source_target_pairs={{0,2},{1,3},{2,0},{3,1},{4,6},{5,7},{6,4},{7,5},{8,10},{9,11},{10,... | collective-permute-start | bytes 1179656 | tf_op jit(solution)/shard_map/ppermute | solution.py:354
  66.5 43.2 %collective-permute-start.20 = (bf16[3,8,64,128]{3,2,1,0:T(8,128)(2,1)S(1)}, bf16[3,8,64,128]{3,2,1,0:T(8,128)(2,1)S(1)}, u32[]{:S(2)}, u32[]{:S(2)}) collective-permute-start(bf16[3,8,64,128]{3,2,1,0:T(8,128)(2,1)S(1)} %get-tuple-element.54), channel_id=1, source_target_pairs={{0,8},{1,9},{2,10},{3,11},{4,12},{5,13},{6,14},{7,15},{8,0},{9,1},... | collective-permute-start | bytes 1179656 | tf_op jit(solution)/shard_map/ppermute | solution.py:354
  67.7 42.0 %collective-permute-start.14 = (bf16[3,8,64,128]{3,2,1,0:T(8,128)(2,1)S(1)}, bf16[3,8,64,128]{3,2,1,0:T(8,128)(2,1)S(1)}, u32[]{:S(2)}, u32[]{:S(2)}) collective-permute-start(bf16[3,8,64,128]{3,2,1,0:T(8,128)(2,1)S(1)} %get-tuple-element.48), channel_id=1, source_target_pairs={{0,10},{1,11},{2,8},{3,9},{4,14},{5,15},{6,12},{7,13},{8,2},{9,3},... | collective-permute-start | bytes 1179656 | tf_op jit(solution)/shard_map/ppermute | solution.py:354
  67.7 49.3 %collective-permute-start.15 = (bf16[3,8,64,128]{3,2,1,0:T(8,128)(2,1)S(1)}, bf16[3,8,64,128]{3,2,1,0:T(8,128)(2,1)S(1)}, u32[]{:S(2)}, u32[]{:S(2)}) collective-permute-start(bf16[3,8,64,128]{3,2,1,0:T(8,128)(2,1)S(1)} %get-tuple-element.49), channel_id=1, source_target_pairs={{0,6},{1,7},{2,4},{3,5},{4,10},{5,11},{6,8},{7,9},{8,14},{9,15},{1... | collective-permute-start | bytes 1179656 | tf_op jit(solution)/shard_map/ppermute | solution.py:354
  109.7 22.5 %collective-permute-start.16 = (bf16[3,8,64,128]{3,2,1,0:T(8,128)(2,1)S(1)}, bf16[3,8,64,128]{3,2,1,0:T(8,128)(2,1)S(1)}, u32[]{:S(2)}, u32[]{:S(2)}) collective-permute-start(bf16[3,8,64,128]{3,2,1,0:T(8,128)(2,1)S(1)} %get-tuple-element.50), channel_id=1, source_target_pairs={{0,9},{1,10},{2,11},{3,8},{4,13},{5,14},{6,15},{7,12},{8,1},{9,2},... | collective-permute-start | bytes 1179656 | tf_op jit(solution)/shard_map/ppermute | solution.py:354
  109.7 22.5 %collective-permute-start.17 = (bf16[3,8,64,128]{3,2,1,0:T(8,128)(2,1)S(1)}, bf16[3,8,64,128]{3,2,1,0:T(8,128)(2,1)S(1)}, u32[]{:S(2)}, u32[]{:S(2)}) collective-permute-start(bf16[3,8,64,128]{3,2,1,0:T(8,128)(2,1)S(1)} %get-tuple-element.51), channel_id=1, source_target_pairs={{0,14},{1,15},{2,12},{3,13},{4,2},{5,3},{6,0},{7,1},{8,6},{9,7},{1... | collective-permute-start | bytes 1179656 | tf_op jit(solution)/shard_map/ppermute | solution.py:354
  109.7 30.3 %collective-permute-start.6 = (bf16[3,8,64,128]{3,2,1,0:T(8,128)(2,1)S(1)}, bf16[3,8,64,128]{3,2,1,0:T(8,128)(2,1)S(1)}, u32[]{:S(2)}, u32[]{:S(2)}) collective-permute-start(bf16[3,8,64,128]{3,2,1,0:T(8,128)(2,1)S(1)} %get-tuple-element.39), channel_id=1, source_target_pairs={{0,1},{1,2},{2,3},{3,0},{4,5},{5,6},{6,7},{7,4},{8,9},{9,10},{10,1... | collective-permute-start | bytes 1179656 | tf_op jit(solution)/shard_map/ppermute | solution.py:354
  109.8 28.9 %collective-permute-start.13 = (bf16[3,8,64,128]{3,2,1,0:T(8,128)(2,1)S(1)}, bf16[3,8,64,128]{3,2,1,0:T(8,128)(2,1)S(1)}, u32[]{:S(2)}, u32[]{:S(2)}) collective-permute-start(bf16[3,8,64,128]{3,2,1,0:T(8,128)(2,1)S(1)} %get-tuple-element.46), channel_id=1, source_target_pairs={{0,13},{1,14},{2,15},{3,12},{4,1},{5,2},{6,3},{7,0},{8,5},{9,6},{1... | collective-permute-start | bytes 1179656 | tf_op jit(solution)/shard_map/ppermute | solution.py:354
  117.0 23.0 %collective-permute-start.7 = (bf16[3,8,64,128]{3,2,1,0:T(8,128)(2,1)S(1)}, bf16[3,8,64,128]{3,2,1,0:T(8,128)(2,1)S(1)}, u32[]{:S(2)}, u32[]{:S(2)}) collective-permute-start(bf16[3,8,64,128]{3,2,1,0:T(8,128)(2,1)S(1)} %get-tuple-element.40), channel_id=1, source_target_pairs={{0,3},{1,0},{2,1},{3,2},{4,7},{5,4},{6,5},{7,6},{8,11},{9,8},{10,9... | collective-permute-start | bytes 1179656 | tf_op jit(solution)/shard_map/ppermute | solution.py:354
  132.2 9.0 %collective-permute-start.8 = (bf16[3,8,64,128]{3,2,1,0:T(8,128)(2,1)S(1)}, bf16[3,8,64,128]{3,2,1,0:T(8,128)(2,1)S(1)}, u32[]{:S(2)}, u32[]{:S(2)}) collective-permute-start(bf16[3,8,64,128]{3,2,1,0:T(8,128)(2,1)S(1)} %get-tuple-element.41), channel_id=1, source_target_pairs={{0,4},{1,5},{2,6},{3,7},{4,8},{5,9},{6,10},{7,11},{8,12},{9,13},{1... | collective-permute-start | bytes 1179656 | tf_op jit(solution)/shard_map/ppermute | solution.py:354
  132.2 9.0 %collective-permute-start.9 = (bf16[3,8,64,128]{3,2,1,0:T(8,128)(2,1)S(1)}, bf16[3,8,64,128]{3,2,1,0:T(8,128)(2,1)S(1)}, u32[]{:S(2)}, u32[]{:S(2)}) collective-permute-start(bf16[3,8,64,128]{3,2,1,0:T(8,128)(2,1)S(1)} %get-tuple-element.42), channel_id=1, source_target_pairs={{0,12},{1,13},{2,14},{3,15},{4,0},{5,1},{6,2},{7,3},{8,4},{9,5},{1... | collective-permute-start | bytes 1179656 | tf_op jit(solution)/shard_map/ppermute | solution.py:354
  (8 other events, 67.6 us)

commit v2 on v1

--- a/solution.py
+++ b/solution.py
@@ -11,13 +11,13 @@
 MIB = 1 << 20
 
 
-WAYS = (
-    (2, 2), (1, 2), (2, 1), (3, 2), (2, 3), (0, 2), (2, 0),
-    (1, 1), (3, 3), (1, 3), (3, 1), (0, 1), (0, 3), (1, 0), (3, 0),
+SETS = 4
+STEPS = (2, 1, 3)
+GROUPS = (
+    tuple((k, i) for k in (0, 1) for i in range(4)),
+    tuple((k, i) for k in (2, 3) for i in (0, 1, 3)),
+    tuple((k, 2) for k in (2, 3)),
 )
-ORDER = WAYS + ((0, 0),)
-FIRST = 4
-GROUPS = ((15, 0, 1, 2, 3, 4, 5, 6), (7, 8, 9, 10), (11, 12, 13, 14))
 
 
 def away(row, way):
@@ -163,20 +163,25 @@
     return jnp.asarray((c % combos == n // LANES) & (c < 3 * combos), BF16)
 
 
-def divide(first, pick, scales, sources, outs):
+def divide(which, pick, scales, sources, outs):
     experts, _, lanes = sources[0].shape
-    for k, out in enumerate(outs):
-        to = away(lax.axis_index("rows"), ORDER[first + k])
-        rows = pl.ds(pl.multiple_of(to * out.shape[2], out.shape[2]), out.shape[2])
-        for t, source in enumerate(sources):
-            combos = slice(t * experts * lanes, (t + 1) * experts * lanes)
-            scale = jnp.dot(scales[rows, :], pick[:, combos], preferred_element_type=F32)
-            for e in range(experts):
-                part = slice(e * lanes, (e + 1) * lanes)
-                out[t, e] = (source[e, rows, :] / scale[:, part]).astype(BF16)
-
-
-def first_kernel(pick, a, b, c, d, tg, tu, td, scale, kept, scales, *outs):
+    _, _, share, width, _ = outs[0].shape
+    for step, out in zip((0,) + STEPS, outs):
+        for i in range(4):
+            way = (i, step) if which % 2 == 0 else (step, i)
+            to = away(lax.axis_index("rows"), way)
+            rows = pl.ds(pl.multiple_of(to * width, width), width)
+            for t, source in enumerate(sources):
+                first = (t * experts + which * share) * lanes
+                combos = slice(first, first + share * lanes)
+                scale = jnp.dot(scales[rows, :], pick[:, combos], preferred_element_type=F32)
+                for e in range(share):
+                    part = slice(e * lanes, (e + 1) * lanes)
+                    x = source[which * share + e, rows, :]
+                    out[i, t, e] = (x / scale[:, part]).astype(BF16)
+
+
+def first_kernel(sets, pick, a, b, c, d, tg, tu, td, scale, kept, scales, *outs):
     sums, groups, _ = scale.shape
     root = jnp.sqrt((a[:sums] + b[:sums]) + (c[:sums] + d[:sums]))
     scale[...] = root
@@ -187,79 +192,100 @@
     for g in range(groups):
         block = jnp.concatenate(in_three(root[:, g, :]) + [rest], axis=0)
         scales[g * LANES : (g + 1) * LANES] = block.T.astype(BF16)
-    divide(0, pick, scales, (tg, tu, td), outs)
-
-
-def rest_kernel(first, pick, scales, tg, tu, td, *outs):
-    divide(first, pick, scales, (tg, tu, td), outs)
-
-
-def scaled(pick, parts, tg, tu, td, ends):
+    for k, which in enumerate(sets):
+        divide(which, pick, scales, (tg, tu, td), outs[4 * k : 4 * k + 4])
+
+
+def rest_kernel(sets, pick, scales, tg, tu, td, *outs):
+    for k, which in enumerate(sets):
+        divide(which, pick, scales, (tg, tu, td), outs[4 * k : 4 * k + 4])
+
+
+def scaled(pick, parts, tg, tu, td):
     experts, width, rows = tg.shape
-    peers = len(ORDER)
     sums = 3 * experts
-    piece = pltpu.VMEM((3, experts, width // peers, rows), BF16)
-    size = 3 * experts * (width // peers) * rows
+    piece = pltpu.VMEM((4, 3, experts // SETS, width // 16, rows), BF16)
     outs = [
         jax.ShapeDtypeStruct((sums, *parts[0].shape[1:]), F32),
         jax.ShapeDtypeStruct((4 * (parts[0].shape[0] - sums), *parts[0].shape[1:]), F32),
         pltpu.VMEM((width, LANES), BF16),
     ]
-    moved = lambda count: 6 * count * size
+    spent = cost(3 * tg.size, 9 * tg.size)
+    params = pltpu.CompilerParams(vmem_limit_bytes=8 * MIB)
     scale, kept, scales, *pieces = pl.pallas_call(
-        first_kernel,
+        lambda *refs: first_kernel((0, 1), *refs),
         in_specs=[VMEM] * 8,
-        out_specs=[VMEM] * (3 + ends[0]),
-        out_shape=outs + [piece] * ends[0],
-        compiler_params=pltpu.CompilerParams(vmem_limit_bytes=8 * MIB),
-        cost_estimate=cost(6 * size * ends[0], moved(ends[0])),
+        out_specs=[VMEM] * 11,
+        out_shape=outs + [piece] * 8,
+        compiler_params=params,
+        cost_estimate=spent,
         name="scale_0",
     )(pick, *parts, tg, tu, td)
-    for first, end in zip(ends, ends[1:]):
-        pieces += pl.pallas_call(
-            lambda *refs, first=first: rest_kernel(first, *refs),
-            in_specs=[VMEM] * 5,
-            out_specs=[VMEM] * (end - first),
-            out_shape=[piece] * (end - first),
-            compiler_params=pltpu.CompilerParams(vmem_limit_bytes=8 * MIB),
-            cost_estimate=cost(6 * size * (end - first), moved(end - first)),
-        )(pick, scales, tg, tu, td)
-    return scale, kept, pieces
-
-
-def place_kernel(ways, *refs):
-    count = len(ways)
-    pieces, outs, done = refs[:count], refs[-4:-1], refs[-1]
+    pieces += pl.pallas_call(
+        lambda *refs: rest_kernel((2, 3), *refs),
+        in_specs=[VMEM] * 5,
+        out_specs=[VMEM] * 8,
+        out_shape=[piece] * 8,
+        compiler_params=params,
+        cost_estimate=spent,
+        name="scale_2",
+    )(pick, scales, tg, tu, td)
+    return scale, kept, [pieces[4 * k : 4 * k + 4] for k in range(SETS)]
+
+
+def turn_corner_kernel(*refs):
+    came, outs = refs[:4], refs[4:]
+    for i, out in enumerate(outs):
+        for j in range(4):
+            out[j] = came[j][i]
+
+
+def turn_corner(came):
+    out = pltpu.VMEM(came[0].shape, BF16)
+    return pl.pallas_call(
+        turn_corner_kernel,
+        in_specs=[VMEM] * 4,
+        out_specs=[VMEM] * 4,
+        out_shape=[out] * 4,
+        compiler_params=pltpu.CompilerParams(vmem_limit_bytes=4 * MIB),
+        cost_estimate=cost(0, 16 * came[0].size),
+    )(*came)
+
+
+def place_kernel(picks, *refs):
+    outs, done = refs[-4:-1], refs[-1]
     copies = []
-    for k, piece in enumerate(pieces):
-        back = [-step for step in ways[k]]
-        came_from = away(lax.axis_index("rows"), back)
-        columns = pl.ds(pl.multiple_of(came_from * LANES, LANES), LANES)
-        for t, out in enumerate(outs):
-            copies.append(pltpu.make_async_copy(piece.at[t], out.at[:, :, columns], done.at[k, t]))
+    for n, ((which, i), came) in enumerate(zip(picks, refs)):
+        _, _, share, _, lanes = came.shape
+        for j, step in enumerate((0,) + STEPS):
+            back = (-i, -step) if which % 2 == 0 else (-step, -i)
+            sender = away(lax.axis_index("rows"), back)
+            columns = pl.ds(pl.multiple_of(sender * lanes, lanes), lanes)
+            for t, out in enumerate(outs):
+                to = out.at[which * share : (which + 1) * share, :, columns]
+                copies.append(pltpu.make_async_copy(came.at[j, t], to, done.at[4 * n + j, t]))
     for copy in copies:
         copy.start()
     for copy in copies:
         copy.wait()
 
 
-def side_by_side(pieces, groups):
-    _, experts, rows, lanes = pieces[0].shape
-    out = pltpu.HBM((experts, rows, len(ORDER) * lanes), BF16)
+def side_by_side(sets, groups):
+    _, _, share, rows, lanes = sets[0][0].shape
+    out = pltpu.HBM((SETS * share, rows, 16 * lanes), BF16)
     so_far = ()
-    for group in groups:
-        count = len(group)
-        ways = [ORDER[k] for k in group]
+    for picks in groups:
+        n = len(picks)
         so_far = pl.pallas_call(
-            lambda *refs, ways=ways: place_kernel(ways, *refs),
-            in_specs=[VMEM] * count + [ANY] * len(so_far),
+            lambda *refs, picks=picks: place_kernel(picks, *refs),
+            in_specs=[VMEM] * n + [ANY] * len(so_far),
             out_specs=[ANY] * 3,
             out_shape=[out] * 3,
-            scratch_shapes=[pltpu.SemaphoreType.DMA((count, 3))],
-            input_output_aliases={count + t: t for t in range(len(so_far))},
+            scratch_shapes=[pltpu.SemaphoreType.DMA((4 * n, 3))],
+            input_output_aliases={n + t: t for t in range(len(so_far))},
             compiler_params=pltpu.CompilerParams(vmem_limit_bytes=8 * MIB),
-            cost_estimate=cost(0, 4 * count * pieces[0].size),
-        )(*[pieces[k] for k in group], *so_far)
+            cost_estimate=cost(0, 4 * n * sets[0][0].size),
+        )(*[sets[which][i] for which, i in picks], *so_far)
     return so_far
 
 
@@ -348,11 +374,19 @@
     tg = turned(mg, sg)
     tu = turned(mu, su)
     td = merged(md, sd)
-    scale, pieces, send = scaled(picker(sums), far, tg, tu, td, (FIRST, 16))
+    scale, pieces, send = scaled(picker(sums), far, tg, tu, td)
+    ways = {k: (pairs((0, k)), pairs((k, 0))) for k in STEPS}
+    half = [[parts[0]] for parts in send]
+    for k, step in sent_in_order():
+        part = send[k][1 + STEPS.index(step)]
+        half[k].append(lax.ppermute(part, "rows", ways[step][k % 2]))
     came = []
-    for k, way in enumerate(WAYS):
-        came.append(lax.ppermute(send[k], "rows", pairs(way)))
-    came.append(send[-1])
+    for k in range(SETS):
+        parts = turn_corner(half[k])
+        whole = [parts[0]] * 4
+        for step in STEPS:
+            whole[step] = lax.ppermute(parts[step], "rows", ways[step][1 - k % 2])
+        came.append(whole)
     columns = placed_by(order_rows_kernel, (pieces,), (8, 16 * LANES))
     columns = from_all(columns, "owner", ALONG_X)
     other = lax.ppermute(placed_by(stack_kernel, columns, (4, 8, 16 * LANES)), "owner", OTHER_CORE)
@@ -360,6 +394,10 @@
     mine = own_scales(scale, experts)
     g, u, d = side_by_side(came, GROUPS)
     return (jnp.swapaxes(g, 1, 2), jnp.swapaxes(u, 1, 2), d, mine[0], mine[1], mine[2], router)
+
+
+def sent_in_order(steps=STEPS):
+    return [(k + i, step) for k in range(0, SETS, 2) for step in steps for i in (0, 1)]
 
 
 def solution(mesh):

time: 144 us -> 145 us (level); the launches traced: 142 us -> 145 us
  Pallas kernels: 19.3 us -> 20.9 us
    ppermute x15 -> x24, waiting for transfers between devices: 61.9 us -> 55.9 us  [the longest x12 32.6 us: body(): whole[step] = lax.ppermute(parts[step], 'rows', ways[step][1 - k % 2])]
    ppermute x9, waiting for transfers between devices: 10.8 us -> 15.3 us  [from_all(): came.append(lax.ppermute(a, axis, way))]
    ppermute x9, starting transfers between devices: 14.7 us -> 16.6 us  [from_all(): came.append(lax.ppermute(a, axis, way))]
    pallas_call x5 -> x9, Pallas kernels: 6.66 us -> 8.3 us  [the longest x3 5.57 us: side_by_side(): pl.pallas_call(lambda *refs, picks=picks: place_kernel(picks, *refs), in_...]
    ppermute x15 -> x24, starting transfers between devices: 31.9 us -> 30.8 us  [the longest x12 18.4 us: body(): half[k].append(lax.ppermute(part, 'rows', ways[step][k % 2]))]
  transfers between devices with their start and end apart: 25 -> 34, of which waited for: 10 -> 18; matrix products, arithmetic and copies ran while one was open for 0% -> 0% of each run, Pallas kernels for 7% -> 7%
where the time goes in v2:
time: 145 us
  waiting for transfers between devices  72.6 us (50%)
  starting transfers between devices  47.5 us (33%)
  Pallas kernels  20.9 us (14%)
  local copies, waits for them, and re-layouts  2.97 us (2%)
    ppermute x12, waiting for transfers between devices, body(): whole[step] = lax.ppermute(parts[step], 'rows', ways[step][1 - k % 2])  32.6 us
    ppermute x12, waiting for transfers between devices, body(): half[k].append(lax.ppermute(part, 'rows', ways[step][k % 2]))  23.3 us
    ppermute x12, starting transfers between devices, body(): half[k].append(lax.ppermute(part, 'rows', ways[step][k % 2]))  18.4 us
    ppermute x9, starting transfers between devices, from_all(): came.append(lax.ppermute(a, axis, way))  16.6 us
    ppermute x9, waiting for transfers between devices, from_all(): came.append(lax.ppermute(a, axis, way))  15.3 us
    ppermute x12, starting transfers between devices, body(): whole[step] = lax.ppermute(parts[step], 'rows', ways[step][1 - k % 2])  12.4 us
    pallas_call x1, Pallas kernels, local_sums(): pl.pallas_call(sums_kernel, in_specs=[ANY] * 8, out_specs=VMEM, out_shape...  7.45 us
    pallas_call x3, Pallas kernels, side_by_side(): pl.pallas_call(lambda *refs, picks=picks: place_kernel(picks, *refs), in_...  5.57 us
  transfers between devices with their start and end apart: 34, of which 18 were waited for; matrix products, arithmetic and copies ran while one was open for 0% of the time, Pallas kernels for 7%

profile of v2, /device:TPU:0, one launch (start us, length us, event | category | flops | bytes accessed | tf_op | source)
XLA Modules:
  0.0 145.0 jit_solution(11334393869718279933)
XLA Ops:
  0.7 7.4 %sums.1.refs_0_ = f32[25,8,128]{2,1,0:T(8,128)S(1)} custom-call(f32[8,128,1024]{2,1,0:T(8,128)} %m.3, bf16[8,128,1024]{2,1,0:T(8,128)(2,1)} %s.3, f32[8,128,1024]{2,1,0:T(8,128)} %m.4, bf16[8,128,1024]{2,1,0:T(8,128)(2,1)} %s.4, f32[8,1024,128]{2,1,0:T(8,128)} %m.5, bf16[8,1024,128]{2,1,0:T(8,128)(2,1)} %s.5, f32[8,128]{1,0:T(8,128)} %bitcast.8, ...), custom_call_target="tpu_custom_call" | custom-call | flops 9437184 | bytes 18874368 | tf_op jit(solution)/shard_map/sums/pallas_call | solution.py:85
  8.1 3.2 %collective-permute-start.2 = (f32[25,8,128]{2,1,0:T(8,128)S(1)}, f32[25,8,128]{2,1,0:T(8,128)S(1)}, u32[]{:S(2)}, u32[]{:S(2)}) collective-permute-start(f32[25,8,128]{2,1,0:T(8,128)S(1)} %sums.1.refs_0_), channel_id=1, source_target_pairs={{0,3},{1,0},{2,1},{3,2},{4,7},{5,4},{6,5},{7,6},{8,11},{9,8},{10,9... | collective-permute-start | bytes 307208 | tf_op jit(solution)/shard_map/ppermute | solution.py:363
  12.9 2.8 %collective-permute-done.2.refs_3_ = f32[25,8,128]{2,1,0:T(8,128)S(1)} collective-permute-done((f32[25,8,128]{2,1,0:T(8,128)S(1)}, f32[25,8,128]{2,1,0:T(8,128)S(1)}, u32[]{:S(2)}, u32[]{:S(2)}) %collective-permute-start.2) | collective-permute-done | bytes 102432 | tf_op jit(solution)/shard_map/ppermute | solution.py:363
  15.7 2.6 %collective-permute-done.1.refs_2_ = f32[25,8,128]{2,1,0:T(8,128)S(1)} collective-permute-done((f32[25,8,128]{2,1,0:T(8,128)S(1)}, f32[25,8,128]{2,1,0:T(8,128)S(1)}, u32[]{:S(2)}, u32[]{:S(2)}) %collective-permute-start.1) | collective-permute-done | bytes 102432 | tf_op jit(solution)/shard_map/ppermute | solution.py:363
  19.4 4.1 %collective-permute-start.5 = (f32[28,8,128]{2,1,0:T(8,128)S(1)}, f32[28,8,128]{2,1,0:T(8,128)S(1)}, u32[]{:S(2)}, u32[]{:S(2)}) collective-permute-start(f32[28,8,128]{2,1,0:T(8,128)S(1)} %shard_map.144.refs_1_), channel_id=1, source_target_pairs={{0,12},{1,13},{2,14},{3,15},{4,0},{5,1},{6,2},{7,3},{8,4},{9,5},{1... | collective-permute-start | bytes 344072 | tf_op jit(solution)/shard_map/ppermute | solution.py:363
  35.3 2.5 %collective-permute-start.8 = (bf16[4,3,2,64,128]{4,3,2,1,0:T(8,128)(2,1)S(1)}, bf16[4,3,2,64,128]{4,3,2,1,0:T(8,128)(2,1)S(1)}, u32[]{:S(2)}, u32[]{:S(2)}) collective-permute-start(bf16[4,3,2,64,128]{4,3,2,1,0:T(8,128)(2,1)S(1)} %get-tuple-element.58), channel_id=1, source_target_pairs={{0,3},{1,0},{2,1},{3,2},{4,7},{5,4},{6,5},{7,6},{8,11},{9,8},{10,9... | collective-permute-start | bytes 1179656 | tf_op jit(solution)/shard_map/ppermute | solution.py:382
  39.5 2.8 %collective-permute-start.32 = (bf16[8,2048]{1,0:T(8,128)(2,1)S(1)}, bf16[8,2048]{1,0:T(8,128)(2,1)S(1)}, u32[]{:S(2)}, u32[]{:S(2)}) collective-permute-start(bf16[8,2048]{1,0:T(8,128)(2,1)S(1)} %shard_map.154.a), channel_id=1, source_target_pairs={{0,96},{16,112},{32,0},{48,16},{64,32},{80,48},{96,64},{112,80},{1... | collective-permute-start | bytes 98312 | tf_op jit(solution)/shard_map/ppermute | solution.py:363
  44.0 2.6 %collective-permute-start.31 = (bf16[8,2048]{1,0:T(8,128)(2,1)S(1)}, bf16[8,2048]{1,0:T(8,128)(2,1)S(1)}, u32[]{:S(2)}, u32[]{:S(2)}) collective-permute-start(bf16[8,2048]{1,0:T(8,128)(2,1)S(1)} %shard_map.154.a), channel_id=1, source_target_pairs={{0,64},{16,80},{32,96},{48,112},{64,0},{80,16},{96,32},{112,48},{1... | collective-permute-start | bytes 98312 | tf_op jit(solution)/shard_map/ppermute | solution.py:363
  46.6 2.8 %collective-permute-done.31.c = bf16[8,2048]{1,0:T(8,128)(2,1)S(1)} collective-permute-done((bf16[8,2048]{1,0:T(8,128)(2,1)S(1)}, bf16[8,2048]{1,0:T(8,128)(2,1)S(1)}, u32[]{:S(2)}, u32[]{:S(2)}) %collective-permute-start.31) | collective-permute-done | bytes 32800 | tf_op jit(solution)/shard_map/ppermute | solution.py:363
  50.4 4.4 %collective-permute-done.30.b = bf16[8,2048]{1,0:T(8,128)(2,1)S(1)} collective-permute-done((bf16[8,2048]{1,0:T(8,128)(2,1)S(1)}, bf16[8,2048]{1,0:T(8,128)(2,1)S(1)}, u32[]{:S(2)}, u32[]{:S(2)}) %collective-permute-start.30) | collective-permute-done | bytes 32800 | tf_op jit(solution)/shard_map/ppermute | solution.py:363
  56.3 3.2 %collective-permute-start.20 = (bf16[4,3,2,64,128]{4,3,2,1,0:T(8,128)(2,1)S(1)}, bf16[4,3,2,64,128]{4,3,2,1,0:T(8,128)(2,1)S(1)}, u32[]{:S(2)}, u32[]{:S(2)}) collective-permute-start(bf16[4,3,2,64,128]{4,3,2,1,0:T(8,128)(2,1)S(1)} %get-tuple-element.74), channel_id=1, source_target_pairs={{0,3},{1,0},{2,1},{3,2},{4,7},{5,4},{6,5},{7,6},{8,11},{9,8},{10,9... | collective-permute-start | bytes 1179656 | tf_op jit(solution)/shard_map/ppermute | solution.py:382
  66.4 5.2 %collective-permute-done.19.refs_2_ = bf16[4,3,2,64,128]{4,3,2,1,0:T(8,128)(2,1)S(1)} collective-permute-done((bf16[4,3,2,64,128]{4,3,2,1,0:T(8,128)(2,1)S(1)}, bf16[4,3,2,64,128]{4,3,2,1,0:T(8,128)(2,1)S(1)}, u32[]{:S(2)}, u32[]{:S(2)}) %collective-permute-start.19) | collective-permute-done | bytes 393248 | tf_op jit(solution)/shard_map/ppermute | solution.py:382
  73.7 2.7 %collective-permute-start.12 = (bf16[4,3,2,64,128]{4,3,2,1,0:T(8,128)(2,1)S(1)}, bf16[4,3,2,64,128]{4,3,2,1,0:T(8,128)(2,1)S(1)}, u32[]{:S(2)}, u32[]{:S(2)}) collective-permute-start(bf16[4,3,2,64,128]{4,3,2,1,0:T(8,128)(2,1)S(1)} %get-tuple-element.63), channel_id=1, source_target_pairs={{0,12},{1,13},{2,14},{3,15},{4,0},{5,1},{6,2},{7,3},{8,4},{9,5},{1... | collective-permute-start | bytes 1179656 | tf_op jit(solution)/shard_map/ppermute | solution.py:382
  76.5 5.1 %collective-permute-done.25.refs_2_ = bf16[4,3,2,64,128]{4,3,2,1,0:T(8,128)(2,1)S(1)} collective-permute-done((bf16[4,3,2,64,128]{4,3,2,1,0:T(8,128)(2,1)S(1)}, bf16[4,3,2,64,128]{4,3,2,1,0:T(8,128)(2,1)S(1)}, u32[]{:S(2)}, u32[]{:S(2)}) %collective-permute-start.25) | collective-permute-done | bytes 393248 | tf_op jit(solution)/shard_map/ppermute | solution.py:382
  83.8 6.1 %collective-permute-done.10.refs_1_ = bf16[4,3,2,64,128]{4,3,2,1,0:T(8,128)(2,1)S(1)} collective-permute-done((bf16[4,3,2,64,128]{4,3,2,1,0:T(8,128)(2,1)S(1)}, bf16[4,3,2,64,128]{4,3,2,1,0:T(8,128)(2,1)S(1)}, u32[]{:S(2)}, u32[]{:S(2)}) %collective-permute-start.10) | collective-permute-done | bytes 393248 | tf_op jit(solution)/shard_map/ppermute | solution.py:382
  92.1 4.9 %collective-permute-done.11.refs_2_ = bf16[4,3,2,64,128]{4,3,2,1,0:T(8,128)(2,1)S(1)} collective-permute-done((bf16[4,3,2,64,128]{4,3,2,1,0:T(8,128)(2,1)S(1)}, bf16[4,3,2,64,128]{4,3,2,1,0:T(8,128)(2,1)S(1)}, u32[]{:S(2)}, u32[]{:S(2)}) %collective-permute-start.11) | collective-permute-done | bytes 393248 | tf_op jit(solution)/shard_map/ppermute | solution.py:382
  98.9 6.5 %collective-permute-done.14.refs_1_ = bf16[4,3,2,64,128]{4,3,2,1,0:T(8,128)(2,1)S(1)} collective-permute-done((bf16[4,3,2,64,128]{4,3,2,1,0:T(8,128)(2,1)S(1)}, bf16[4,3,2,64,128]{4,3,2,1,0:T(8,128)(2,1)S(1)}, u32[]{:S(2)}, u32[]{:S(2)}) %collective-permute-start.14) | collective-permute-done | bytes 393248 | tf_op jit(solution)/shard_map/ppermute | solution.py:388
  106.0 9.0 %collective-permute-done.21.refs_1_ = bf16[4,3,2,64,128]{4,3,2,1,0:T(8,128)(2,1)S(1)} collective-permute-done((bf16[4,3,2,64,128]{4,3,2,1,0:T(8,128)(2,1)S(1)}, bf16[4,3,2,64,128]{4,3,2,1,0:T(8,128)(2,1)S(1)}, u32[]{:S(2)}, u32[]{:S(2)}) %collective-permute-start.21) | collective-permute-done | bytes 393248 | tf_op jit(solution)/shard_map/ppermute | solution.py:388
  115.2 7.0 %collective-permute-done.22.refs_2_ = bf16[4,3,2,64,128]{4,3,2,1,0:T(8,128)(2,1)S(1)} collective-permute-done((bf16[4,3,2,64,128]{4,3,2,1,0:T(8,128)(2,1)S(1)}, bf16[4,3,2,64,128]{4,3,2,1,0:T(8,128)(2,1)S(1)}, u32[]{:S(2)}, u32[]{:S(2)}) %collective-permute-start.22) | collective-permute-done | bytes 393248 | tf_op jit(solution)/shard_map/ppermute | solution.py:388
  122.3 3.2 %collective-permute-start.17 = (bf16[4,3,2,64,128]{4,3,2,1,0:T(8,128)(2,1)S(1)}, bf16[4,3,2,64,128]{4,3,2,1,0:T(8,128)(2,1)S(1)}, u32[]{:S(2)}, u32[]{:S(2)}) collective-permute-start(bf16[4,3,2,64,128]{4,3,2,1,0:T(8,128)(2,1)S(1)} %get-tuple-element.70), channel_id=1, source_target_pairs={{0,3},{1,0},{2,1},{3,2},{4,7},{5,4},{6,5},{7,6},{8,11},{9,8},{10,9... | collective-permute-start | bytes 1179656 | tf_op jit(solution)/shard_map/ppermute | solution.py:388
  125.5 2.2 %collective-permute-start.9 = (bf16[4,3,2,64,128]{4,3,2,1,0:T(8,128)(2,1)S(1)}, bf16[4,3,2,64,128]{4,3,2,1,0:T(8,128)(2,1)S(1)}, u32[]{:S(2)}, u32[]{:S(2)}) collective-permute-start(bf16[4,3,2,64,128]{4,3,2,1,0:T(8,128)(2,1)S(1)} %get-tuple-element.59), channel_id=1, source_target_pairs={{0,8},{1,9},{2,10},{3,11},{4,12},{5,13},{6,14},{7,15},{8,0},{9,1},... | collective-permute-start | bytes 1179656 | tf_op jit(solution)/shard_map/ppermute | solution.py:388
  129.2 2.5 %shard_map.151 = (bf16[8,64,2048]{2,1,0:T(8,128)(2,1)}, bf16[8,64,2048]{2,1,0:T(8,128)(2,1)}, bf16[8,64,2048]{2,1,0:T(8,128)(2,1)}) custom-call(bf16[4,3,2,64,128]{4,3,2,1,0:T(8,128)(2,1)S(1)} %get-tuple-element.75.refs_0_, bf16[4,3,2,64,128]{4,3,2,1,0:T(8,128)(2,1)S(1)} %collective-permute-done.21.refs_1_, ...), custom_call_target="tpu_custom_call" | custom-call | bytes 6291456 | tf_op jit(solution)/shard_map/pallas_call | solution.py:279
  131.6 2.6 %collective-permute-done.15.refs_2_ = bf16[4,3,2,64,128]{4,3,2,1,0:T(8,128)(2,1)S(1)} collective-permute-done((bf16[4,3,2,64,128]{4,3,2,1,0:T(8,128)(2,1)S(1)}, bf16[4,3,2,64,128]{4,3,2,1,0:T(8,128)(2,1)S(1)}, u32[]{:S(2)}, u32[]{:S(2)}) %collective-permute-start.15) | collective-permute-done | bytes 393248 | tf_op jit(solution)/shard_map/ppermute | solution.py:388
  134.2 7.4 %collective-permute-done.16.refs_4_ = bf16[4,3,2,64,128]{4,3,2,1,0:T(8,128)(2,1)S(1)} collective-permute-done((bf16[4,3,2,64,128]{4,3,2,1,0:T(8,128)(2,1)S(1)}, bf16[4,3,2,64,128]{4,3,2,1,0:T(8,128)(2,1)S(1)}, u32[]{:S(2)}, u32[]{:S(2)}) %collective-permute-start.16) | collective-permute-done | bytes 393248 | tf_op jit(solution)/shard_map/ppermute | solution.py:388
  (76 shorter events, 41.1 us)
Async XLA Ops:
  19.4 12.1 %collective-permute-start.5 = (f32[28,8,128]{2,1,0:T(8,128)S(1)}, f32[28,8,128]{2,1,0:T(8,128)S(1)}, u32[]{:S(2)}, u32[]{:S(2)}) collective-permute-start(f32[28,8,128]{2,1,0:T(8,128)S(1)} %shard_map.144.refs_1_), channel_id=1, source_target_pairs={{0,12},{1,13},{2,14},{3,15},{4,0},{5,1},{6,2},{7,3},{8,4},{9,5},{1... | collective-permute-start | bytes 344072 | tf_op jit(solution)/shard_map/ppermute | solution.py:363
  33.9 22.4 %collective-permute-start.6 = (bf16[4,3,2,64,128]{4,3,2,1,0:T(8,128)(2,1)S(1)}, bf16[4,3,2,64,128]{4,3,2,1,0:T(8,128)(2,1)S(1)}, u32[]{:S(2)}, u32[]{:S(2)}) collective-permute-start(bf16[4,3,2,64,128]{4,3,2,1,0:T(8,128)(2,1)S(1)} %get-tuple-element.56), channel_id=1, source_target_pairs={{0,2},{1,3},{2,0},{3,1},{4,6},{5,7},{6,4},{7,5},{8,10},{9,11},{10,... | collective-permute-start | bytes 1179656 | tf_op jit(solution)/shard_map/ppermute | solution.py:382
  34.6 24.9 %collective-permute-start.7 = (bf16[4,3,2,64,128]{4,3,2,1,0:T(8,128)(2,1)S(1)}, bf16[4,3,2,64,128]{4,3,2,1,0:T(8,128)(2,1)S(1)}, u32[]{:S(2)}, u32[]{:S(2)}) collective-permute-start(bf16[4,3,2,64,128]{4,3,2,1,0:T(8,128)(2,1)S(1)} %get-tuple-element.57), channel_id=1, source_target_pairs={{0,1},{1,2},{2,3},{3,0},{4,5},{5,6},{6,7},{7,4},{8,9},{9,10},{10,1... | collective-permute-start | bytes 1179656 | tf_op jit(solution)/shard_map/ppermute | solution.py:382
  35.3 26.4 %collective-permute-start.8 = (bf16[4,3,2,64,128]{4,3,2,1,0:T(8,128)(2,1)S(1)}, bf16[4,3,2,64,128]{4,3,2,1,0:T(8,128)(2,1)S(1)}, u32[]{:S(2)}, u32[]{:S(2)}) collective-permute-start(bf16[4,3,2,64,128]{4,3,2,1,0:T(8,128)(2,1)S(1)} %get-tuple-element.58), channel_id=1, source_target_pairs={{0,3},{1,0},{2,1},{3,2},{4,7},{5,4},{6,5},{7,6},{8,11},{9,8},{10,9... | collective-permute-start | bytes 1179656 | tf_op jit(solution)/shard_map/ppermute | solution.py:382
  37.8 26.5 %collective-permute-start.18 = (bf16[4,3,2,64,128]{4,3,2,1,0:T(8,128)(2,1)S(1)}, bf16[4,3,2,64,128]{4,3,2,1,0:T(8,128)(2,1)S(1)}, u32[]{:S(2)}, u32[]{:S(2)}) collective-permute-start(bf16[4,3,2,64,128]{4,3,2,1,0:T(8,128)(2,1)S(1)} %get-tuple-element.72), channel_id=1, source_target_pairs={{0,2},{1,3},{2,0},{3,1},{4,6},{5,7},{6,4},{7,5},{8,10},{9,11},{10,... | collective-permute-start | bytes 1179656 | tf_op jit(solution)/shard_map/ppermute | solution.py:382
  56.3 15.3 %collective-permute-start.19 = (bf16[4,3,2,64,128]{4,3,2,1,0:T(8,128)(2,1)S(1)}, bf16[4,3,2,64,128]{4,3,2,1,0:T(8,128)(2,1)S(1)}, u32[]{:S(2)}, u32[]{:S(2)}) collective-permute-start(bf16[4,3,2,64,128]{4,3,2,1,0:T(8,128)(2,1)S(1)} %get-tuple-element.73), channel_id=1, source_target_pairs={{0,1},{1,2},{2,3},{3,0},{4,5},{5,6},{6,7},{7,4},{8,9},{9,10},{10,1... | collective-permute-start | bytes 1179656 | tf_op jit(solution)/shard_map/ppermute | solution.py:382
  56.3 16.8 %collective-permute-start.20 = (bf16[4,3,2,64,128]{4,3,2,1,0:T(8,128)(2,1)S(1)}, bf16[4,3,2,64,128]{4,3,2,1,0:T(8,128)(2,1)S(1)}, u32[]{:S(2)}, u32[]{:S(2)}) collective-permute-start(bf16[4,3,2,64,128]{4,3,2,1,0:T(8,128)(2,1)S(1)} %get-tuple-element.74), channel_id=1, source_target_pairs={{0,3},{1,0},{2,1},{3,2},{4,7},{5,4},{6,5},{7,6},{8,11},{9,8},{10,9... | collective-permute-start | bytes 1179656 | tf_op jit(solution)/shard_map/ppermute | solution.py:382
  59.5 14.2 %collective-permute-start.24 = (bf16[4,3,2,64,128]{4,3,2,1,0:T(8,128)(2,1)S(1)}, bf16[4,3,2,64,128]{4,3,2,1,0:T(8,128)(2,1)S(1)}, u32[]{:S(2)}, u32[]{:S(2)}) collective-permute-start(bf16[4,3,2,64,128]{4,3,2,1,0:T(8,128)(2,1)S(1)} %get-tuple-element.80), channel_id=1, source_target_pairs={{0,8},{1,9},{2,10},{3,11},{4,12},{5,13},{6,14},{7,15},{8,0},{9,1},... | collective-permute-start | bytes 1179656 | tf_op jit(solution)/shard_map/ppermute | solution.py:382
  61.7 19.8 %collective-permute-start.25 = (bf16[4,3,2,64,128]{4,3,2,1,0:T(8,128)(2,1)S(1)}, bf16[4,3,2,64,128]{4,3,2,1,0:T(8,128)(2,1)S(1)}, u32[]{:S(2)}, u32[]{:S(2)}) collective-permute-start(bf16[4,3,2,64,128]{4,3,2,1,0:T(8,128)(2,1)S(1)} %get-tuple-element.81), channel_id=1, source_target_pairs={{0,4},{1,5},{2,6},{3,7},{4,8},{5,9},{6,10},{7,11},{8,12},{9,13},{1... | collective-permute-start | bytes 1179656 | tf_op jit(solution)/shard_map/ppermute | solution.py:382
  64.3 17.8 %collective-permute-start.26 = (bf16[4,3,2,64,128]{4,3,2,1,0:T(8,128)(2,1)S(1)}, bf16[4,3,2,64,128]{4,3,2,1,0:T(8,128)(2,1)S(1)}, u32[]{:S(2)}, u32[]{:S(2)}) collective-permute-start(bf16[4,3,2,64,128]{4,3,2,1,0:T(8,128)(2,1)S(1)} %get-tuple-element.82), channel_id=1, source_target_pairs={{0,12},{1,13},{2,14},{3,15},{4,0},{5,1},{6,2},{7,3},{8,4},{9,5},{1... | collective-permute-start | bytes 1179656 | tf_op jit(solution)/shard_map/ppermute | solution.py:382
  71.5 18.4 %collective-permute-start.10 = (bf16[4,3,2,64,128]{4,3,2,1,0:T(8,128)(2,1)S(1)}, bf16[4,3,2,64,128]{4,3,2,1,0:T(8,128)(2,1)S(1)}, u32[]{:S(2)}, u32[]{:S(2)}) collective-permute-start(bf16[4,3,2,64,128]{4,3,2,1,0:T(8,128)(2,1)S(1)} %get-tuple-element.61), channel_id=1, source_target_pairs={{0,8},{1,9},{2,10},{3,11},{4,12},{5,13},{6,14},{7,15},{8,0},{9,1},... | collective-permute-start | bytes 1179656 | tf_op jit(solution)/shard_map/ppermute | solution.py:382
  73.1 23.9 %collective-permute-start.11 = (bf16[4,3,2,64,128]{4,3,2,1,0:T(8,128)(2,1)S(1)}, bf16[4,3,2,64,128]{4,3,2,1,0:T(8,128)(2,1)S(1)}, u32[]{:S(2)}, u32[]{:S(2)}) collective-permute-start(bf16[4,3,2,64,128]{4,3,2,1,0:T(8,128)(2,1)S(1)} %get-tuple-element.62), channel_id=1, source_target_pairs={{0,4},{1,5},{2,6},{3,7},{4,8},{5,9},{6,10},{7,11},{8,12},{9,13},{1... | collective-permute-start | bytes 1179656 | tf_op jit(solution)/shard_map/ppermute | solution.py:382
  73.7 25.2 %collective-permute-start.12 = (bf16[4,3,2,64,128]{4,3,2,1,0:T(8,128)(2,1)S(1)}, bf16[4,3,2,64,128]{4,3,2,1,0:T(8,128)(2,1)S(1)}, u32[]{:S(2)}, u32[]{:S(2)}) collective-permute-start(bf16[4,3,2,64,128]{4,3,2,1,0:T(8,128)(2,1)S(1)} %get-tuple-element.63), channel_id=1, source_target_pairs={{0,12},{1,13},{2,14},{3,15},{4,0},{5,1},{6,2},{7,3},{8,4},{9,5},{1... | collective-permute-start | bytes 1179656 | tf_op jit(solution)/shard_map/ppermute | solution.py:382
  81.5 23.9 %collective-permute-start.14 = (bf16[4,3,2,64,128]{4,3,2,1,0:T(8,128)(2,1)S(1)}, bf16[4,3,2,64,128]{4,3,2,1,0:T(8,128)(2,1)S(1)}, u32[]{:S(2)}, u32[]{:S(2)}) collective-permute-start(bf16[4,3,2,64,128]{4,3,2,1,0:T(8,128)(2,1)S(1)} %get-tuple-element.66), channel_id=1, source_target_pairs={{0,4},{1,5},{2,6},{3,7},{4,8},{5,9},{6,10},{7,11},{8,12},{9,13},{1... | collective-permute-start | bytes 1179656 | tf_op jit(solution)/shard_map/ppermute | solution.py:388
  82.1 32.9 %collective-permute-start.21 = (bf16[4,3,2,64,128]{4,3,2,1,0:T(8,128)(2,1)S(1)}, bf16[4,3,2,64,128]{4,3,2,1,0:T(8,128)(2,1)S(1)}, u32[]{:S(2)}, u32[]{:S(2)}) collective-permute-start(bf16[4,3,2,64,128]{4,3,2,1,0:T(8,128)(2,1)S(1)} %get-tuple-element.76), channel_id=1, source_target_pairs={{0,4},{1,5},{2,6},{3,7},{4,8},{5,9},{6,10},{7,11},{8,12},{9,13},{1... | collective-permute-start | bytes 1179656 | tf_op jit(solution)/shard_map/ppermute | solution.py:388
  89.9 32.3 %collective-permute-start.22 = (bf16[4,3,2,64,128]{4,3,2,1,0:T(8,128)(2,1)S(1)}, bf16[4,3,2,64,128]{4,3,2,1,0:T(8,128)(2,1)S(1)}, u32[]{:S(2)}, u32[]{:S(2)}) collective-permute-start(bf16[4,3,2,64,128]{4,3,2,1,0:T(8,128)(2,1)S(1)} %get-tuple-element.77), channel_id=1, source_target_pairs={{0,8},{1,9},{2,10},{3,11},{4,12},{5,13},{6,14},{7,15},{8,0},{9,1},... | collective-permute-start | bytes 1179656 | tf_op jit(solution)/shard_map/ppermute | solution.py:388
  97.0 25.3 %collective-permute-start.23 = (bf16[4,3,2,64,128]{4,3,2,1,0:T(8,128)(2,1)S(1)}, bf16[4,3,2,64,128]{4,3,2,1,0:T(8,128)(2,1)S(1)}, u32[]{:S(2)}, u32[]{:S(2)}) collective-permute-start(bf16[4,3,2,64,128]{4,3,2,1,0:T(8,128)(2,1)S(1)} %get-tuple-element.78), channel_id=1, source_target_pairs={{0,12},{1,13},{2,14},{3,15},{4,0},{5,1},{6,2},{7,3},{8,4},{9,5},{1... | collective-permute-start | bytes 1179656 | tf_op jit(solution)/shard_map/ppermute | solution.py:388
  98.9 23.4 %collective-permute-start.27 = (bf16[4,3,2,64,128]{4,3,2,1,0:T(8,128)(2,1)S(1)}, bf16[4,3,2,64,128]{4,3,2,1,0:T(8,128)(2,1)S(1)}, u32[]{:S(2)}, u32[]{:S(2)}) collective-permute-start(bf16[4,3,2,64,128]{4,3,2,1,0:T(8,128)(2,1)S(1)} %get-tuple-element.84), channel_id=1, source_target_pairs={{0,1},{1,2},{2,3},{3,0},{4,5},{5,6},{6,7},{7,4},{8,9},{9,10},{10,1... | collective-permute-start | bytes 1179656 | tf_op jit(solution)/shard_map/ppermute | solution.py:388
  105.4 20.1 %collective-permute-start.28 = (bf16[4,3,2,64,128]{4,3,2,1,0:T(8,128)(2,1)S(1)}, bf16[4,3,2,64,128]{4,3,2,1,0:T(8,128)(2,1)S(1)}, u32[]{:S(2)}, u32[]{:S(2)}) collective-permute-start(bf16[4,3,2,64,128]{4,3,2,1,0:T(8,128)(2,1)S(1)} %get-tuple-element.85), channel_id=1, source_target_pairs={{0,2},{1,3},{2,0},{3,1},{4,6},{5,7},{6,4},{7,5},{8,10},{9,11},{10,... | collective-permute-start | bytes 1179656 | tf_op jit(solution)/shard_map/ppermute | solution.py:388
  115.0 12.7 %collective-permute-start.29 = (bf16[4,3,2,64,128]{4,3,2,1,0:T(8,128)(2,1)S(1)}, bf16[4,3,2,64,128]{4,3,2,1,0:T(8,128)(2,1)S(1)}, u32[]{:S(2)}, u32[]{:S(2)}) collective-permute-start(bf16[4,3,2,64,128]{4,3,2,1,0:T(8,128)(2,1)S(1)} %get-tuple-element.86), channel_id=1, source_target_pairs={{0,3},{1,0},{2,1},{3,2},{4,7},{5,4},{6,5},{7,6},{8,11},{9,8},{10,9... | collective-permute-start | bytes 1179656 | tf_op jit(solution)/shard_map/ppermute | solution.py:388
  122.3 19.4 %collective-permute-start.16 = (bf16[4,3,2,64,128]{4,3,2,1,0:T(8,128)(2,1)S(1)}, bf16[4,3,2,64,128]{4,3,2,1,0:T(8,128)(2,1)S(1)}, u32[]{:S(2)}, u32[]{:S(2)}) collective-permute-start(bf16[4,3,2,64,128]{4,3,2,1,0:T(8,128)(2,1)S(1)} %get-tuple-element.69), channel_id=1, source_target_pairs={{0,1},{1,2},{2,3},{3,0},{4,5},{5,6},{6,7},{7,4},{8,9},{9,10},{10,1... | collective-permute-start | bytes 1179656 | tf_op jit(solution)/shard_map/ppermute | solution.py:388
  122.3 19.4 %collective-permute-start.17 = (bf16[4,3,2,64,128]{4,3,2,1,0:T(8,128)(2,1)S(1)}, bf16[4,3,2,64,128]{4,3,2,1,0:T(8,128)(2,1)S(1)}, u32[]{:S(2)}, u32[]{:S(2)}) collective-permute-start(bf16[4,3,2,64,128]{4,3,2,1,0:T(8,128)(2,1)S(1)} %get-tuple-element.70), channel_id=1, source_target_pairs={{0,3},{1,0},{2,1},{3,2},{4,7},{5,4},{6,5},{7,6},{8,11},{9,8},{10,9... | collective-permute-start | bytes 1179656 | tf_op jit(solution)/shard_map/ppermute | solution.py:388
  125.5 18.2 %collective-permute-start.9 = (bf16[4,3,2,64,128]{4,3,2,1,0:T(8,128)(2,1)S(1)}, bf16[4,3,2,64,128]{4,3,2,1,0:T(8,128)(2,1)S(1)}, u32[]{:S(2)}, u32[]{:S(2)}) collective-permute-start(bf16[4,3,2,64,128]{4,3,2,1,0:T(8,128)(2,1)S(1)} %get-tuple-element.59), channel_id=1, source_target_pairs={{0,8},{1,9},{2,10},{3,11},{4,12},{5,13},{6,14},{7,15},{8,0},{9,1},... | collective-permute-start | bytes 1179656 | tf_op jit(solution)/shard_map/ppermute | solution.py:388
  127.7 15.9 %collective-permute-start.13 = (bf16[4,3,2,64,128]{4,3,2,1,0:T(8,128)(2,1)S(1)}, bf16[4,3,2,64,128]{4,3,2,1,0:T(8,128)(2,1)S(1)}, u32[]{:S(2)}, u32[]{:S(2)}) collective-permute-start(bf16[4,3,2,64,128]{4,3,2,1,0:T(8,128)(2,1)S(1)} %get-tuple-element.64), channel_id=1, source_target_pairs={{0,2},{1,3},{2,0},{3,1},{4,6},{5,7},{6,4},{7,5},{8,10},{9,11},{10,... | collective-permute-start | bytes 1179656 | tf_op jit(solution)/shard_map/ppermute | solution.py:388
  (17 other events, 129.7 us)

commit v3 on v2

--- a/solution.py
+++ b/solution.py
@@ -11,12 +11,16 @@
 MIB = 1 << 20
 
 
-SETS = 4
+SHARES = (3, 3, 1, 1)
+STARTS = (0, 3, 6, 7)
+SETS = len(SHARES)
 STEPS = (2, 1, 3)
+NEAR = (0, 2, 1, 3)
 GROUPS = (
-    tuple((k, i) for k in (0, 1) for i in range(4)),
-    tuple((k, i) for k in (2, 3) for i in (0, 1, 3)),
-    tuple((k, 2) for k in (2, 3)),
+    tuple((k, 0) for k in range(SETS)),
+    ((0, 1), (1, 1), (0, 3), (1, 3)),
+    ((0, 2), (1, 2), (2, 1), (3, 1), (2, 3), (3, 3)),
+    ((2, 2), (3, 2)),
 )
 
 
@@ -34,7 +38,8 @@
 
 
 def sums_kernel(*refs):
-    sources, out, held, columns, arrived = refs[:8], refs[8], refs[9:17], refs[17], refs[18]
+    sources, out, merged, held = refs[:8], refs[8], refs[9:12], refs[12:20]
+    columns, arrived = refs[20], refs[21]
     experts = sources[0].shape[0]
     groups = sources[4].shape[1] // LANES
     small = [
@@ -63,11 +68,13 @@
             for g in range(groups):
                 part = slice(g * LANES, (g + 1) * LANES)
                 x = m[e, :, part] + s[e, :, part].astype(F32)
+                merged[t][e, :, part] = x
                 out[t * experts + e, g : g + 1, :] = jnp.sum(x * x, axis=0, keepdims=True)
         so_far = columns[...]
         for g in range(groups):
             part = slice(g * LANES, (g + 1) * LANES)
             x = held[4][e, part] + held[5][e, part].astype(F32)
+            merged[2][e, part] = x
             total = jnp.sum(x * x, axis=1, keepdims=True)
             so_far = jnp.where(lane == e * groups + g, total, so_far)
         columns[...] = so_far
@@ -85,52 +92,33 @@
     return pl.pallas_call(
         sums_kernel,
         in_specs=[ANY] * 8,
-        out_specs=VMEM,
-        out_shape=jax.ShapeDtypeStruct((3 * experts + 1, width // LANES, LANES), F32),
+        out_specs=[VMEM] * 4,
+        out_shape=[jax.ShapeDtypeStruct((3 * experts + 1, width // LANES, LANES), F32)]
+        + [pltpu.VMEM(a.shape, F32) for a in (mg, mu, md)],
         scratch_shapes=[pltpu.VMEM(a.shape, a.dtype) for a in arrays]
         + [pltpu.VMEM((LANES, LANES), F32), pltpu.SemaphoreType.DMA((7, experts))],
-        compiler_params=pltpu.CompilerParams(vmem_limit_bytes=24 * MIB),
+        compiler_params=pltpu.CompilerParams(vmem_limit_bytes=20 * MIB),
         cost_estimate=cost(9 * mg.size, 18 * mg.size),
         name="sums",
     )(*arrays)
 
 
-def turn_kernel(m, s, out):
-    x = m[0] + s[0].astype(F32)
-    for g in range(x.shape[1] // LANES):
-        out[0, g * LANES : (g + 1) * LANES, :] = x[:, g * LANES : (g + 1) * LANES].T
-
-
-def turned(m, s):
+def turn_kernel(m, out):
+    for g in range(m.shape[2] // LANES):
+        out[0, g * LANES : (g + 1) * LANES, :] = m[0, :, g * LANES : (g + 1) * LANES].T
+
+
+def turned(m):
     experts, rows, width = m.shape
-    tall = pl.BlockSpec((1, rows, width), lambda e: (e, 0, 0))
     return pl.pallas_call(
         turn_kernel,
         grid=(experts,),
-        in_specs=[tall, tall],
+        in_specs=[pl.BlockSpec((1, rows, width), lambda e: (e, 0, 0))],
         out_specs=pl.BlockSpec((1, width, rows), lambda e: (e, 0, 0)),
         out_shape=jax.ShapeDtypeStruct((experts, width, rows), F32),
         compiler_params=pltpu.CompilerParams(vmem_limit_bytes=8 * MIB),
-        cost_estimate=cost(8 * m.size, 10 * m.size),
-    )(m, s)
-
-
-def merge_kernel(m, s, out):
-    out[...] = m[...] + s[...].astype(F32)
-
-
-def merged(m, s):
-    flat = pl.BlockSpec((1, *m.shape[1:]), lambda e: (e, 0, 0))
-    return pl.pallas_call(
-        merge_kernel,
-        grid=(m.shape[0],),
-        in_specs=[flat, flat],
-        out_specs=flat,
-        out_shape=jax.ShapeDtypeStruct(m.shape, F32),
-        compiler_params=pltpu.CompilerParams(vmem_limit_bytes=8 * MIB),
-        cost_estimate=cost(2 * m.size, 10 * m.size),
-        name="merge_down",
-    )(m, s)
+        cost_estimate=cost(8 * m.size, 8 * m.size),
+    )(m)
 
 
 def fold_kernel(sums, a, b, c, d, out):
@@ -163,25 +151,25 @@
     return jnp.asarray((c % combos == n // LANES) & (c < 3 * combos), BF16)
 
 
-def divide(which, pick, scales, sources, outs):
+def divide(picks, pick, scales, sources, outs):
     experts, _, lanes = sources[0].shape
-    _, _, share, width, _ = outs[0].shape
-    for step, out in zip((0,) + STEPS, outs):
+    for (which, step), out in zip(picks, outs):
+        _, _, share, width, _ = out.shape
         for i in range(4):
             way = (i, step) if which % 2 == 0 else (step, i)
             to = away(lax.axis_index("rows"), way)
             rows = pl.ds(pl.multiple_of(to * width, width), width)
             for t, source in enumerate(sources):
-                first = (t * experts + which * share) * lanes
+                first = (t * experts + STARTS[which]) * lanes
                 combos = slice(first, first + share * lanes)
                 scale = jnp.dot(scales[rows, :], pick[:, combos], preferred_element_type=F32)
                 for e in range(share):
                     part = slice(e * lanes, (e + 1) * lanes)
-                    x = source[which * share + e, rows, :]
+                    x = source[STARTS[which] + e, rows, :]
                     out[i, t, e] = (x / scale[:, part]).astype(BF16)
 
 
-def first_kernel(sets, pick, a, b, c, d, tg, tu, td, scale, kept, scales, *outs):
+def first_kernel(picks, pick, a, b, c, d, tg, tu, td, scale, kept, scales, *outs):
     sums, groups, _ = scale.shape
     root = jnp.sqrt((a[:sums] + b[:sums]) + (c[:sums] + d[:sums]))
     scale[...] = root
@@ -192,19 +180,19 @@
     for g in range(groups):
         block = jnp.concatenate(in_three(root[:, g, :]) + [rest], axis=0)
         scales[g * LANES : (g + 1) * LANES] = block.T.astype(BF16)
-    for k, which in enumerate(sets):
-        divide(which, pick, scales, (tg, tu, td), outs[4 * k : 4 * k + 4])
-
-
-def rest_kernel(sets, pick, scales, tg, tu, td, *outs):
-    for k, which in enumerate(sets):
-        divide(which, pick, scales, (tg, tu, td), outs[4 * k : 4 * k + 4])
+    divide(picks, pick, scales, (tg, tu, td), outs)
+
+
+def rest_kernel(picks, pick, scales, tg, tu, td, *outs):
+    divide(picks, pick, scales, (tg, tu, td), outs)
 
 
 def scaled(pick, parts, tg, tu, td):
     experts, width, rows = tg.shape
     sums = 3 * experts
-    piece = pltpu.VMEM((4, 3, experts // SETS, width // 16, rows), BF16)
+    made = lambda k: pltpu.VMEM((4, 3, SHARES[k], width // 16, rows), BF16)
+    early = [(k, STEPS[0]) for k in (0, 1)]
+    late = [(k, step) for k in range(SETS) for step in STEPS + (0,) if (k, step) not in early]
     outs = [
         jax.ShapeDtypeStruct((sums, *parts[0].shape[1:]), F32),
         jax.ShapeDtypeStruct((4 * (parts[0].shape[0] - sums), *parts[0].shape[1:]), F32),
@@ -213,24 +201,24 @@
     spent = cost(3 * tg.size, 9 * tg.size)
     params = pltpu.CompilerParams(vmem_limit_bytes=8 * MIB)
     scale, kept, scales, *pieces = pl.pallas_call(
-        lambda *refs: first_kernel((0, 1), *refs),
+        lambda *refs: first_kernel(early, *refs),
         in_specs=[VMEM] * 8,
-        out_specs=[VMEM] * 11,
-        out_shape=outs + [piece] * 8,
+        out_specs=[VMEM] * (3 + len(early)),
+        out_shape=outs + [made(k) for k, _ in early],
         compiler_params=params,
         cost_estimate=spent,
         name="scale_0",
     )(pick, *parts, tg, tu, td)
     pieces += pl.pallas_call(
-        lambda *refs: rest_kernel((2, 3), *refs),
+        lambda *refs: rest_kernel(late, *refs),
         in_specs=[VMEM] * 5,
-        out_specs=[VMEM] * 8,
-        out_shape=[piece] * 8,
+        out_specs=[VMEM] * len(late),
+        out_shape=[made(k) for k, _ in late],
         compiler_params=params,
         cost_estimate=spent,
         name="scale_2",
     )(pick, scales, tg, tu, td)
-    return scale, kept, [pieces[4 * k : 4 * k + 4] for k in range(SETS)]
+    return scale, kept, dict(zip(early + late, pieces))
 
 
 def turn_corner_kernel(*refs):
@@ -262,7 +250,7 @@
             sender = away(lax.axis_index("rows"), back)
             columns = pl.ds(pl.multiple_of(sender * lanes, lanes), lanes)
             for t, out in enumerate(outs):
-                to = out.at[which * share : (which + 1) * share, :, columns]
+                to = out.at[STARTS[which] : STARTS[which] + share, :, columns]
                 copies.append(pltpu.make_async_copy(came.at[j, t], to, done.at[4 * n + j, t]))
     for copy in copies:
         copy.start()
@@ -271,8 +259,8 @@
 
 
 def side_by_side(sets, groups):
-    _, _, share, rows, lanes = sets[0][0].shape
-    out = pltpu.HBM((SETS * share, rows, 16 * lanes), BF16)
+    _, _, _, rows, lanes = sets[0][0].shape
+    out = pltpu.HBM((sum(SHARES), rows, 16 * lanes), BF16)
     so_far = ()
     for picks in groups:
         n = len(picks)
@@ -292,7 +280,7 @@
 def order_rows_kernel(pieces, out):
     for a in range(4):
         for b in range(4):
-            place = away(lax.axis_index("rows"), (-a, -b))
+            place = away(lax.axis_index("rows"), (-NEAR[a], -NEAR[b]))
             out[:, pl.ds(pl.multiple_of(place * LANES, LANES), LANES)] = pieces[4 * a + b].astype(BF16)
 
 
@@ -351,8 +339,8 @@
     return [(i, (i // 4 + way[0]) % 4 * 4 + (i % 4 + way[1]) % 4) for i in range(16)]
 
 
-ALONG_Y = [pairs((0, k)) for k in (1, 2, 3)]
-ALONG_Z = [pairs((k, 0)) for k in (1, 2, 3)]
+ALONG_Y = [pairs((0, k)) for k in NEAR[1:]]
+ALONG_Z = [pairs((k, 0)) for k in NEAR[1:]]
 ALONG_X = [[(i, (i // 2 + k) % 4 * 2 + i % 2) for i in range(8)] for k in (1, 2, 3)]
 OTHER_CORE = [(i, i ^ 1) for i in range(8)]
 
@@ -367,19 +355,17 @@
 def body(mg, sg, mu, su, md, sd, w, gain):
     experts = mg.shape[0]
     sums = 3 * experts
-    here = local_sums(*[in_hbm(a) for a in (mg, sg, mu, su, md, sd, w.T, gain[None, :])])
+    here, gate, up, td = local_sums(*[in_hbm(a) for a in (mg, sg, mu, su, md, sd, w.T, gain[None, :])])
     near = from_all(here, "rows", ALONG_Y)
     line = folded(sums, near)
     far = from_all(line, "rows", ALONG_Z)
-    tg = turned(mg, sg)
-    tu = turned(mu, su)
-    td = merged(md, sd)
+    tg = turned(gate)
+    tu = turned(up)
     scale, pieces, send = scaled(picker(sums), far, tg, tu, td)
     ways = {k: (pairs((0, k)), pairs((k, 0))) for k in STEPS}
-    half = [[parts[0]] for parts in send]
+    half = [[send[k, 0]] for k in range(SETS)]
     for k, step in sent_in_order():
-        part = send[k][1 + STEPS.index(step)]
-        half[k].append(lax.ppermute(part, "rows", ways[step][k % 2]))
+        half[k].append(lax.ppermute(send[k, step], "rows", ways[step][k % 2]))
     came = []
     for k in range(SETS):
         parts = turn_corner(half[k])

time: 145 us -> 167 us (1.15); the launches traced: 145 us -> 164 us
  waiting for transfers between devices: 72.6 us -> 103 us
  starting transfers between devices: 47.5 us -> 37.8 us
  local copies, waits for them, and re-layouts: 2.97 us -> 0.01 us
    ppermute x12, waiting for transfers between devices: 23.3 us -> 50.3 us  [body(): half[k].append(lax.ppermute(send[k, step], 'rows', ways[step][k % 2]))]
    ppermute x12, waiting for transfers between devices: 32.6 us -> 40.3 us  [body(): whole[step] = lax.ppermute(parts[step], 'rows', ways[step][1 - k % 2])]
    ppermute x12, starting transfers between devices: 18.4 us -> 12.1 us  [body(): half[k].append(lax.ppermute(send[k, step], 'rows', ways[step][k % 2]))]
    unnamed x14 -> x2, local copies, waits for them, and re-layouts: 2.97 us -> 0.01 us
    ppermute x12, starting transfers between devices: 12.4 us -> 9.65 us  [body(): whole[step] = lax.ppermute(parts[step], 'rows', ways[step][1 - k % 2])]
    ppermute x9, waiting for transfers between devices: 15.3 us -> 12.8 us  [from_all(): came.append(lax.ppermute(a, axis, way))]
    pallas_call x3 -> x4, Pallas kernels: 5.57 us -> 6.18 us  [side_by_side(): pl.pallas_call(lambda *refs, picks=picks: place_kernel(picks, *refs), in_...]
    pallas_call x6 -> x5, Pallas kernels: 13.5 us -> 13.7 us  [the longest x1 7.35 us: local_sums(): pl.pallas_call(sums_kernel, in_specs=[ANY] * 8, out_specs=[VMEM] * 4, out...]
  transfers between devices with their start and end apart: 34 -> 34, of which waited for: 18 -> 15; matrix products, arithmetic and copies ran while one was open for 0% -> 0% of each run, Pallas kernels for 7% -> 6%
where the time goes in v3:
time: 167 us; the launch traced here: 164 us
  waiting for transfers between devices  103 us (62%)
  starting transfers between devices  37.8 us (23%)
  Pallas kernels  21.8 us (13%)
    ppermute x12, waiting for transfers between devices, body(): half[k].append(lax.ppermute(send[k, step], 'rows', ways[step][k % 2]))  50.3 us
    ppermute x12, waiting for transfers between devices, body(): whole[step] = lax.ppermute(parts[step], 'rows', ways[step][1 - k % 2])  40.3 us
    ppermute x9, starting transfers between devices, from_all(): came.append(lax.ppermute(a, axis, way))  16 us
    ppermute x9, waiting for transfers between devices, from_all(): came.append(lax.ppermute(a, axis, way))  12.8 us
    ppermute x12, starting transfers between devices, body(): half[k].append(lax.ppermute(send[k, step], 'rows', ways[step][k % 2]))  12.1 us
    ppermute x12, starting transfers between devices, body(): whole[step] = lax.ppermute(parts[step], 'rows', ways[step][1 - k % 2])  9.65 us
    pallas_call x1, Pallas kernels, local_sums(): pl.pallas_call(sums_kernel, in_specs=[ANY] * 8, out_specs=[VMEM] * 4, out...  7.35 us
    pallas_call x4, Pallas kernels, side_by_side(): pl.pallas_call(lambda *refs, picks=picks: place_kernel(picks, *refs), in_...  6.18 us
  transfers between devices with their start and end apart: 34, of which 15 were waited for; matrix products, arithmetic and copies ran while one was open for 0% of the time, Pallas kernels for 6%

profile of v3, /device:TPU:0, one launch (start us, length us, event | category | flops | bytes accessed | tf_op | source)
XLA Modules:
  0.0 164.0 jit_solution(225825081598232990)
XLA Ops:
  0.6 7.3 %sums.1 = (f32[25,8,128]{2,1,0:T(8,128)S(1)}, f32[8,128,1024]{2,1,0:T(8,128)S(1)}, f32[8,128,1024]{2,1,0:T(8,128)S(1)}, f32[8,1024,128]{2,1,0:T(8,128)S(1)}) custom-call(f32[8,128,1024]{2,1,0:T(8,128)} %refs_0_.3, bf16[8,128,1024]{2,1,0:T(8,128)(2,1)} %refs_1_.1, f32[8,128,1024]{2,1,0:T(8,128)} %refs_2_.1, bf16[8,128,1024]{2,1,0:T(8,128)(2,1)} %refs_3_.1, ...), custom_call_target="tpu_custom_call" | custom-call | flops 9437184 | bytes 18874368 | tf_op jit(solution)/shard_map/sums/pallas_call | solution.py:92
  8.0 3.2 %collective-permute-start.2 = (f32[25,8,128]{2,1,0:T(8,128)S(1)}, f32[25,8,128]{2,1,0:T(8,128)S(1)}, u32[]{:S(2)}, u32[]{:S(2)}) collective-permute-start(f32[25,8,128]{2,1,0:T(8,128)S(1)} %get-tuple-element.61.refs_0_), channel_id=1, source_target_pairs={{0,3},{1,0},{2,1},{3,2},{4,7},{5,4},{6,5},{7,6},{8,11},{9,8},{10,9... | collective-permute-start | bytes 307208 | tf_op jit(solution)/shard_map/ppermute | solution.py:351
  11.2 2.2 %collective-permute-start = (f32[25,8,128]{2,1,0:T(8,128)S(1)}, f32[25,8,128]{2,1,0:T(8,128)S(1)}, u32[]{:S(2)}, u32[]{:S(2)}) collective-permute-start(f32[25,8,128]{2,1,0:T(8,128)S(1)} %get-tuple-element.61.refs_0_), channel_id=1, source_target_pairs={{0,2},{1,3},{2,0},{3,1},{4,6},{5,7},{6,4},{7,5},{8,10},{9,11},{10,... | collective-permute-start | bytes 307208 | tf_op jit(solution)/shard_map/ppermute | solution.py:351
  13.4 5.5 %collective-permute-done.1.refs_2_ = f32[25,8,128]{2,1,0:T(8,128)S(1)} collective-permute-done((f32[25,8,128]{2,1,0:T(8,128)S(1)}, f32[25,8,128]{2,1,0:T(8,128)S(1)}, u32[]{:S(2)}, u32[]{:S(2)}) %collective-permute-start.1) | collective-permute-done | bytes 102432 | tf_op jit(solution)/shard_map/ppermute | solution.py:351
  19.0 4.1 %collective-permute-start.5 = (f32[28,8,128]{2,1,0:T(8,128)S(1)}, f32[28,8,128]{2,1,0:T(8,128)S(1)}, u32[]{:S(2)}, u32[]{:S(2)}) collective-permute-start(f32[28,8,128]{2,1,0:T(8,128)S(1)} %shard_map.144.refs_1_), channel_id=1, source_target_pairs={{0,12},{1,13},{2,14},{3,15},{4,0},{5,1},{6,2},{7,3},{8,4},{9,5},{1... | collective-permute-start | bytes 344072 | tf_op jit(solution)/shard_map/ppermute | solution.py:351
  23.1 1.9 %collective-permute-start.3 = (f32[28,8,128]{2,1,0:T(8,128)S(1)}, f32[28,8,128]{2,1,0:T(8,128)S(1)}, u32[]{:S(2)}, u32[]{:S(2)}) collective-permute-start(f32[28,8,128]{2,1,0:T(8,128)S(1)} %shard_map.144.refs_1_), channel_id=1, source_target_pairs={{0,8},{1,9},{2,10},{3,11},{4,12},{5,13},{6,14},{7,15},{8,0},{9,1},... | collective-permute-start | bytes 344072 | tf_op jit(solution)/shard_map/ppermute | solution.py:351
  28.2 2.1 %collective-permute-done.4.refs_3_ = f32[28,8,128]{2,1,0:T(8,128)S(1)} collective-permute-done((f32[28,8,128]{2,1,0:T(8,128)S(1)}, f32[28,8,128]{2,1,0:T(8,128)S(1)}, u32[]{:S(2)}, u32[]{:S(2)}) %collective-permute-start.4) | collective-permute-done | bytes 114720 | tf_op jit(solution)/shard_map/ppermute | solution.py:351
  31.2 2.2 %scale_2.1 = (bf16[4,3,3,64,128]{4,3,2,1,0:T(8,128)(2,1)S(1)}, bf16[4,3,3,64,128]{4,3,2,1,0:T(8,128)(2,1)S(1)}, bf16[4,3,3,64,128]{4,3,2,1,0:T(8,128)(2,1)S(1)},...) custom-call(bf16[128,3072]{1,0:T(8,128)(2,1)S(1)} %copy-done, ...), custom_call_target="tpu_custom_call" | custom-call | flops 3145728 | bytes 9437184 | tf_op jit(solution)/shard_map/scale_2/pallas_call | solution.py:212
  33.6 3.3 %collective-permute-start.16 = (bf16[4,3,3,64,128]{4,3,2,1,0:T(8,128)(2,1)S(1)}, bf16[4,3,3,64,128]{4,3,2,1,0:T(8,128)(2,1)S(1)}, u32[]{:S(2)}, u32[]{:S(2)}) collective-permute-start(bf16[4,3,3,64,128]{4,3,2,1,0:T(8,128)(2,1)S(1)} %get-tuple-element.79), channel_id=1, source_target_pairs={{0,3},{1,0},{2,1},{3,2},{4,7},{5,4},{6,5},{7,6},{8,11},{9,8},{10,9... | collective-permute-start | bytes 1769480 | tf_op jit(solution)/shard_map/ppermute | solution.py:368
  36.8 2.8 %collective-permute-start.32 = (bf16[8,2048]{1,0:T(8,128)(2,1)S(1)}, bf16[8,2048]{1,0:T(8,128)(2,1)S(1)}, u32[]{:S(2)}, u32[]{:S(2)}) collective-permute-start(bf16[8,2048]{1,0:T(8,128)(2,1)S(1)} %shard_map.155.a), channel_id=1, source_target_pairs={{0,96},{16,112},{32,0},{48,16},{64,32},{80,48},{96,64},{112,80},{1... | collective-permute-start | bytes 98312 | tf_op jit(solution)/shard_map/ppermute | solution.py:351
  42.3 2.8 %collective-permute-done.31.c = bf16[8,2048]{1,0:T(8,128)(2,1)S(1)} collective-permute-done((bf16[8,2048]{1,0:T(8,128)(2,1)S(1)}, bf16[8,2048]{1,0:T(8,128)(2,1)S(1)}, u32[]{:S(2)}, u32[]{:S(2)}) %collective-permute-start.31) | collective-permute-done | bytes 32800 | tf_op jit(solution)/shard_map/ppermute | solution.py:351
  46.7 2.5 %collective-permute-start.6 = (bf16[4,3,1,64,128]{4,3,2,1,0:T(8,128)(2,1)S(1)}, bf16[4,3,1,64,128]{4,3,2,1,0:T(8,128)(2,1)S(1)}, u32[]{:S(2)}, u32[]{:S(2)}) collective-permute-start(bf16[4,3,1,64,128]{4,3,2,1,0:T(8,128)(2,1)S(1)} %get-tuple-element.67), channel_id=1, source_target_pairs={{0,2},{1,3},{2,0},{3,1},{4,6},{5,7},{6,4},{7,5},{8,10},{9,11},{10,... | collective-permute-start | bytes 589832 | tf_op jit(solution)/shard_map/ppermute | solution.py:368
  49.3 16.3 %collective-permute-done.6.refs_1_ = bf16[4,3,1,64,128]{4,3,2,1,0:T(8,128)(2,1)S(1)} collective-permute-done((bf16[4,3,1,64,128]{4,3,2,1,0:T(8,128)(2,1)S(1)}, bf16[4,3,1,64,128]{4,3,2,1,0:T(8,128)(2,1)S(1)}, u32[]{:S(2)}, u32[]{:S(2)}) %collective-permute-start.6) | collective-permute-done | bytes 196640 | tf_op jit(solution)/shard_map/ppermute | solution.py:368
  65.9 1.9 %collective-permute-done.7.refs_2_ = bf16[4,3,1,64,128]{4,3,2,1,0:T(8,128)(2,1)S(1)} collective-permute-done((bf16[4,3,1,64,128]{4,3,2,1,0:T(8,128)(2,1)S(1)}, bf16[4,3,1,64,128]{4,3,2,1,0:T(8,128)(2,1)S(1)}, u32[]{:S(2)}, u32[]{:S(2)}) %collective-permute-start.7) | collective-permute-done | bytes 196640 | tf_op jit(solution)/shard_map/ppermute | solution.py:368
  68.6 2.6 %collective-permute-done.8.refs_3_ = bf16[4,3,1,64,128]{4,3,2,1,0:T(8,128)(2,1)S(1)} collective-permute-done((bf16[4,3,1,64,128]{4,3,2,1,0:T(8,128)(2,1)S(1)}, bf16[4,3,1,64,128]{4,3,2,1,0:T(8,128)(2,1)S(1)}, u32[]{:S(2)}, u32[]{:S(2)}) %collective-permute-start.8) | collective-permute-done | bytes 196640 | tf_op jit(solution)/shard_map/ppermute | solution.py:368
  72.0 2.7 %collective-permute-start.20 = (bf16[4,3,3,64,128]{4,3,2,1,0:T(8,128)(2,1)S(1)}, bf16[4,3,3,64,128]{4,3,2,1,0:T(8,128)(2,1)S(1)}, u32[]{:S(2)}, u32[]{:S(2)}) collective-permute-start(bf16[4,3,3,64,128]{4,3,2,1,0:T(8,128)(2,1)S(1)} %get-tuple-element.84), channel_id=1, source_target_pairs={{0,12},{1,13},{2,14},{3,15},{4,0},{5,1},{6,2},{7,3},{8,4},{9,5},{1... | collective-permute-start | bytes 1769480 | tf_op jit(solution)/shard_map/ppermute | solution.py:368
  76.4 13.4 %collective-permute-done.10.refs_1_ = bf16[4,3,1,64,128]{4,3,2,1,0:T(8,128)(2,1)S(1)} collective-permute-done((bf16[4,3,1,64,128]{4,3,2,1,0:T(8,128)(2,1)S(1)}, bf16[4,3,1,64,128]{4,3,2,1,0:T(8,128)(2,1)S(1)}, u32[]{:S(2)}, u32[]{:S(2)}) %collective-permute-start.10) | collective-permute-done | bytes 196640 | tf_op jit(solution)/shard_map/ppermute | solution.py:368
  89.9 15.4 %collective-permute-done.11.refs_2_ = bf16[4,3,1,64,128]{4,3,2,1,0:T(8,128)(2,1)S(1)} collective-permute-done((bf16[4,3,1,64,128]{4,3,2,1,0:T(8,128)(2,1)S(1)}, bf16[4,3,1,64,128]{4,3,2,1,0:T(8,128)(2,1)S(1)}, u32[]{:S(2)}, u32[]{:S(2)}) %collective-permute-start.11) | collective-permute-done | bytes 196640 | tf_op jit(solution)/shard_map/ppermute | solution.py:368
  106.4 2.8 %collective-permute-start.24 = (bf16[4,3,1,64,128]{4,3,2,1,0:T(8,128)(2,1)S(1)}, bf16[4,3,1,64,128]{4,3,2,1,0:T(8,128)(2,1)S(1)}, u32[]{:S(2)}, u32[]{:S(2)}) collective-permute-start(bf16[4,3,1,64,128]{4,3,2,1,0:T(8,128)(2,1)S(1)} %get-tuple-element.88), channel_id=1, source_target_pairs={{0,12},{1,13},{2,14},{3,15},{4,0},{5,1},{6,2},{7,3},{8,4},{9,5},{1... | collective-permute-start | bytes 589832 | tf_op jit(solution)/shard_map/ppermute | solution.py:374
  111.1 14.0 %collective-permute-done.22.refs_2_ = bf16[4,3,1,64,128]{4,3,2,1,0:T(8,128)(2,1)S(1)} collective-permute-done((bf16[4,3,1,64,128]{4,3,2,1,0:T(8,128)(2,1)S(1)}, bf16[4,3,1,64,128]{4,3,2,1,0:T(8,128)(2,1)S(1)}, u32[]{:S(2)}, u32[]{:S(2)}) %collective-permute-start.22) | collective-permute-done | bytes 196640 | tf_op jit(solution)/shard_map/ppermute | solution.py:374
  125.1 3.2 %collective-permute-start.29 = (bf16[4,3,3,64,128]{4,3,2,1,0:T(8,128)(2,1)S(1)}, bf16[4,3,3,64,128]{4,3,2,1,0:T(8,128)(2,1)S(1)}, u32[]{:S(2)}, u32[]{:S(2)}) collective-permute-start(bf16[4,3,3,64,128]{4,3,2,1,0:T(8,128)(2,1)S(1)} %get-tuple-element.93), channel_id=1, source_target_pairs={{0,3},{1,0},{2,1},{3,2},{4,7},{5,4},{6,5},{7,6},{8,11},{9,8},{10,9... | collective-permute-start | bytes 1769480 | tf_op jit(solution)/shard_map/ppermute | solution.py:374
  129.9 22.6 %collective-permute-done.27.refs_1_ = bf16[4,3,3,64,128]{4,3,2,1,0:T(8,128)(2,1)S(1)} collective-permute-done((bf16[4,3,3,64,128]{4,3,2,1,0:T(8,128)(2,1)S(1)}, bf16[4,3,3,64,128]{4,3,2,1,0:T(8,128)(2,1)S(1)}, u32[]{:S(2)}, u32[]{:S(2)}) %collective-permute-start.27) | collective-permute-done | bytes 589856 | tf_op jit(solution)/shard_map/ppermute | solution.py:374
  152.5 3.2 %collective-permute-done.29.refs_3_ = bf16[4,3,3,64,128]{4,3,2,1,0:T(8,128)(2,1)S(1)} collective-permute-done((bf16[4,3,3,64,128]{4,3,2,1,0:T(8,128)(2,1)S(1)}, bf16[4,3,3,64,128]{4,3,2,1,0:T(8,128)(2,1)S(1)}, u32[]{:S(2)}, u32[]{:S(2)}) %collective-permute-start.29) | collective-permute-done | bytes 589856 | tf_op jit(solution)/shard_map/ppermute | solution.py:374
  160.6 1.9 %shard_map.153 = (bf16[8,64,2048]{2,1,0:T(8,128)(2,1)}, bf16[8,64,2048]{2,1,0:T(8,128)(2,1)}, bf16[8,64,2048]{2,1,0:T(8,128)(2,1)}) custom-call(bf16[4,3,3,64,128]{4,3,2,1,0:T(8,128)(2,1)S(1)} %collective-permute-done.17.refs_0_, ...), custom_call_target="tpu_custom_call", output_to_operand_aliasing={{0}: (6, {}), {1}: (7, {}), {2}: (8, {})} | custom-call | bytes 7077888 | tf_op jit(solution)/shard_map/pallas_call | solution.py:267
  (64 shorter events, 23.1 us)
Async XLA Ops:
  11.2 7.7 %collective-permute-start.1 = (f32[25,8,128]{2,1,0:T(8,128)S(1)}, f32[25,8,128]{2,1,0:T(8,128)S(1)}, u32[]{:S(2)}, u32[]{:S(2)}) collective-permute-start(f32[25,8,128]{2,1,0:T(8,128)S(1)} %get-tuple-element.61.refs_0_), channel_id=1, source_target_pairs={{0,1},{1,2},{2,3},{3,0},{4,5},{5,6},{6,7},{7,4},{8,9},{9,10},{10,1... | collective-permute-start | bytes 307208 | tf_op jit(solution)/shard_map/ppermute | solution.py:351
  19.0 9.3 %collective-permute-start.5 = (f32[28,8,128]{2,1,0:T(8,128)S(1)}, f32[28,8,128]{2,1,0:T(8,128)S(1)}, u32[]{:S(2)}, u32[]{:S(2)}) collective-permute-start(f32[28,8,128]{2,1,0:T(8,128)S(1)} %shard_map.144.refs_1_), channel_id=1, source_target_pairs={{0,12},{1,13},{2,14},{3,15},{4,0},{5,1},{6,2},{7,3},{8,4},{9,5},{1... | collective-permute-start | bytes 344072 | tf_op jit(solution)/shard_map/ppermute | solution.py:351
  33.5 38.5 %collective-permute-start.15 = (bf16[4,3,3,64,128]{4,3,2,1,0:T(8,128)(2,1)S(1)}, bf16[4,3,3,64,128]{4,3,2,1,0:T(8,128)(2,1)S(1)}, u32[]{:S(2)}, u32[]{:S(2)}) collective-permute-start(bf16[4,3,3,64,128]{4,3,2,1,0:T(8,128)(2,1)S(1)} %get-tuple-element.78), channel_id=1, source_target_pairs={{0,1},{1,2},{2,3},{3,0},{4,5},{5,6},{6,7},{7,4},{8,9},{9,10},{10,1... | collective-permute-start | bytes 1769480 | tf_op jit(solution)/shard_map/ppermute | solution.py:368
  33.6 41.1 %collective-permute-start.16 = (bf16[4,3,3,64,128]{4,3,2,1,0:T(8,128)(2,1)S(1)}, bf16[4,3,3,64,128]{4,3,2,1,0:T(8,128)(2,1)S(1)}, u32[]{:S(2)}, u32[]{:S(2)}) collective-permute-start(bf16[4,3,3,64,128]{4,3,2,1,0:T(8,128)(2,1)S(1)} %get-tuple-element.79), channel_id=1, source_target_pairs={{0,3},{1,0},{2,1},{3,2},{4,7},{5,4},{6,5},{7,6},{8,11},{9,8},{10,9... | collective-permute-start | bytes 1769480 | tf_op jit(solution)/shard_map/ppermute | solution.py:368
  39.6 36.7 %collective-permute-start.14 = (bf16[4,3,3,64,128]{4,3,2,1,0:T(8,128)(2,1)S(1)}, bf16[4,3,3,64,128]{4,3,2,1,0:T(8,128)(2,1)S(1)}, u32[]{:S(2)}, u32[]{:S(2)}) collective-permute-start(bf16[4,3,3,64,128]{4,3,2,1,0:T(8,128)(2,1)S(1)} %get-tuple-element.77), channel_id=1, source_target_pairs={{0,2},{1,3},{2,0},{3,1},{4,6},{5,7},{6,4},{7,5},{8,10},{9,11},{10,... | collective-permute-start | bytes 1769480 | tf_op jit(solution)/shard_map/ppermute | solution.py:368
  46.7 18.8 %collective-permute-start.6 = (bf16[4,3,1,64,128]{4,3,2,1,0:T(8,128)(2,1)S(1)}, bf16[4,3,1,64,128]{4,3,2,1,0:T(8,128)(2,1)S(1)}, u32[]{:S(2)}, u32[]{:S(2)}) collective-permute-start(bf16[4,3,1,64,128]{4,3,2,1,0:T(8,128)(2,1)S(1)} %get-tuple-element.67), channel_id=1, source_target_pairs={{0,2},{1,3},{2,0},{3,1},{4,6},{5,7},{6,4},{7,5},{8,10},{9,11},{10,... | collective-permute-start | bytes 589832 | tf_op jit(solution)/shard_map/ppermute | solution.py:368
  49.3 18.6 %collective-permute-start.7 = (bf16[4,3,1,64,128]{4,3,2,1,0:T(8,128)(2,1)S(1)}, bf16[4,3,1,64,128]{4,3,2,1,0:T(8,128)(2,1)S(1)}, u32[]{:S(2)}, u32[]{:S(2)}) collective-permute-start(bf16[4,3,1,64,128]{4,3,2,1,0:T(8,128)(2,1)S(1)} %get-tuple-element.68), channel_id=1, source_target_pairs={{0,1},{1,2},{2,3},{3,0},{4,5},{5,6},{6,7},{7,4},{8,9},{9,10},{10,1... | collective-permute-start | bytes 589832 | tf_op jit(solution)/shard_map/ppermute | solution.py:368
  67.8 38.6 %collective-permute-start.19 = (bf16[4,3,3,64,128]{4,3,2,1,0:T(8,128)(2,1)S(1)}, bf16[4,3,3,64,128]{4,3,2,1,0:T(8,128)(2,1)S(1)}, u32[]{:S(2)}, u32[]{:S(2)}) collective-permute-start(bf16[4,3,3,64,128]{4,3,2,1,0:T(8,128)(2,1)S(1)} %get-tuple-element.83), channel_id=1, source_target_pairs={{0,4},{1,5},{2,6},{3,7},{4,8},{5,9},{6,10},{7,11},{8,12},{9,13},{1... | collective-permute-start | bytes 1769480 | tf_op jit(solution)/shard_map/ppermute | solution.py:368
  71.2 18.7 %collective-permute-start.10 = (bf16[4,3,1,64,128]{4,3,2,1,0:T(8,128)(2,1)S(1)}, bf16[4,3,1,64,128]{4,3,2,1,0:T(8,128)(2,1)S(1)}, u32[]{:S(2)}, u32[]{:S(2)}) collective-permute-start(bf16[4,3,1,64,128]{4,3,2,1,0:T(8,128)(2,1)S(1)} %get-tuple-element.72), channel_id=1, source_target_pairs={{0,8},{1,9},{2,10},{3,11},{4,12},{5,13},{6,14},{7,15},{8,0},{9,1},... | collective-permute-start | bytes 589832 | tf_op jit(solution)/shard_map/ppermute | solution.py:368
  72.0 37.3 %collective-permute-start.20 = (bf16[4,3,3,64,128]{4,3,2,1,0:T(8,128)(2,1)S(1)}, bf16[4,3,3,64,128]{4,3,2,1,0:T(8,128)(2,1)S(1)}, u32[]{:S(2)}, u32[]{:S(2)}) collective-permute-start(bf16[4,3,3,64,128]{4,3,2,1,0:T(8,128)(2,1)S(1)} %get-tuple-element.84), channel_id=1, source_target_pairs={{0,12},{1,13},{2,14},{3,15},{4,0},{5,1},{6,2},{7,3},{8,4},{9,5},{1... | collective-permute-start | bytes 1769480 | tf_op jit(solution)/shard_map/ppermute | solution.py:368
  74.7 34.7 %collective-permute-start.18 = (bf16[4,3,3,64,128]{4,3,2,1,0:T(8,128)(2,1)S(1)}, bf16[4,3,3,64,128]{4,3,2,1,0:T(8,128)(2,1)S(1)}, u32[]{:S(2)}, u32[]{:S(2)}) collective-permute-start(bf16[4,3,3,64,128]{4,3,2,1,0:T(8,128)(2,1)S(1)} %get-tuple-element.82), channel_id=1, source_target_pairs={{0,8},{1,9},{2,10},{3,11},{4,12},{5,13},{6,14},{7,15},{8,0},{9,1},... | collective-permute-start | bytes 1769480 | tf_op jit(solution)/shard_map/ppermute | solution.py:368
  76.3 29.1 %collective-permute-start.11 = (bf16[4,3,1,64,128]{4,3,2,1,0:T(8,128)(2,1)S(1)}, bf16[4,3,1,64,128]{4,3,2,1,0:T(8,128)(2,1)S(1)}, u32[]{:S(2)}, u32[]{:S(2)}) collective-permute-start(bf16[4,3,1,64,128]{4,3,2,1,0:T(8,128)(2,1)S(1)} %get-tuple-element.73), channel_id=1, source_target_pairs={{0,4},{1,5},{2,6},{3,7},{4,8},{5,9},{6,10},{7,11},{8,12},{9,13},{1... | collective-permute-start | bytes 589832 | tf_op jit(solution)/shard_map/ppermute | solution.py:368
  89.9 16.1 %collective-permute-start.12 = (bf16[4,3,1,64,128]{4,3,2,1,0:T(8,128)(2,1)S(1)}, bf16[4,3,1,64,128]{4,3,2,1,0:T(8,128)(2,1)S(1)}, u32[]{:S(2)}, u32[]{:S(2)}) collective-permute-start(bf16[4,3,1,64,128]{4,3,2,1,0:T(8,128)(2,1)S(1)} %get-tuple-element.74), channel_id=1, source_target_pairs={{0,12},{1,13},{2,14},{3,15},{4,0},{5,1},{6,2},{7,3},{8,4},{9,5},{1... | collective-permute-start | bytes 589832 | tf_op jit(solution)/shard_map/ppermute | solution.py:368
  105.3 23.1 %collective-permute-start.26 = (bf16[4,3,3,64,128]{4,3,2,1,0:T(8,128)(2,1)S(1)}, bf16[4,3,3,64,128]{4,3,2,1,0:T(8,128)(2,1)S(1)}, u32[]{:S(2)}, u32[]{:S(2)}) collective-permute-start(bf16[4,3,3,64,128]{4,3,2,1,0:T(8,128)(2,1)S(1)} %get-tuple-element.90), channel_id=1, source_target_pairs={{0,4},{1,5},{2,6},{3,7},{4,8},{5,9},{6,10},{7,11},{8,12},{9,13},{1... | collective-permute-start | bytes 1769480 | tf_op jit(solution)/shard_map/ppermute | solution.py:374
  106.0 19.1 %collective-permute-start.22 = (bf16[4,3,1,64,128]{4,3,2,1,0:T(8,128)(2,1)S(1)}, bf16[4,3,1,64,128]{4,3,2,1,0:T(8,128)(2,1)S(1)}, u32[]{:S(2)}, u32[]{:S(2)}) collective-permute-start(bf16[4,3,1,64,128]{4,3,2,1,0:T(8,128)(2,1)S(1)} %get-tuple-element.86), channel_id=1, source_target_pairs={{0,4},{1,5},{2,6},{3,7},{4,8},{5,9},{6,10},{7,11},{8,12},{9,13},{1... | collective-permute-start | bytes 589832 | tf_op jit(solution)/shard_map/ppermute | solution.py:374
  106.4 18.7 %collective-permute-start.24 = (bf16[4,3,1,64,128]{4,3,2,1,0:T(8,128)(2,1)S(1)}, bf16[4,3,1,64,128]{4,3,2,1,0:T(8,128)(2,1)S(1)}, u32[]{:S(2)}, u32[]{:S(2)}) collective-permute-start(bf16[4,3,1,64,128]{4,3,2,1,0:T(8,128)(2,1)S(1)} %get-tuple-element.88), channel_id=1, source_target_pairs={{0,12},{1,13},{2,14},{3,15},{4,0},{5,1},{6,2},{7,3},{8,4},{9,5},{1... | collective-permute-start | bytes 589832 | tf_op jit(solution)/shard_map/ppermute | solution.py:374
  109.3 19.1 %collective-permute-start.23 = (bf16[4,3,1,64,128]{4,3,2,1,0:T(8,128)(2,1)S(1)}, bf16[4,3,1,64,128]{4,3,2,1,0:T(8,128)(2,1)S(1)}, u32[]{:S(2)}, u32[]{:S(2)}) collective-permute-start(bf16[4,3,1,64,128]{4,3,2,1,0:T(8,128)(2,1)S(1)} %get-tuple-element.87), channel_id=1, source_target_pairs={{0,1},{1,2},{2,3},{3,0},{4,5},{5,6},{6,7},{7,4},{8,9},{9,10},{10,1... | collective-permute-start | bytes 589832 | tf_op jit(solution)/shard_map/ppermute | solution.py:374
  109.4 19.1 %collective-permute-start.28 = (bf16[4,3,3,64,128]{4,3,2,1,0:T(8,128)(2,1)S(1)}, bf16[4,3,3,64,128]{4,3,2,1,0:T(8,128)(2,1)S(1)}, u32[]{:S(2)}, u32[]{:S(2)}) collective-permute-start(bf16[4,3,3,64,128]{4,3,2,1,0:T(8,128)(2,1)S(1)} %get-tuple-element.92), channel_id=1, source_target_pairs={{0,12},{1,13},{2,14},{3,15},{4,0},{5,1},{6,2},{7,3},{8,4},{9,5},{1... | collective-permute-start | bytes 1769480 | tf_op jit(solution)/shard_map/ppermute | solution.py:374
  125.1 27.4 %collective-permute-start.27 = (bf16[4,3,3,64,128]{4,3,2,1,0:T(8,128)(2,1)S(1)}, bf16[4,3,3,64,128]{4,3,2,1,0:T(8,128)(2,1)S(1)}, u32[]{:S(2)}, u32[]{:S(2)}) collective-permute-start(bf16[4,3,3,64,128]{4,3,2,1,0:T(8,128)(2,1)S(1)} %get-tuple-element.91), channel_id=1, source_target_pairs={{0,1},{1,2},{2,3},{3,0},{4,5},{5,6},{6,7},{7,4},{8,9},{9,10},{10,1... | collective-permute-start | bytes 1769480 | tf_op jit(solution)/shard_map/ppermute | solution.py:374
  125.1 30.6 %collective-permute-start.29 = (bf16[4,3,3,64,128]{4,3,2,1,0:T(8,128)(2,1)S(1)}, bf16[4,3,3,64,128]{4,3,2,1,0:T(8,128)(2,1)S(1)}, u32[]{:S(2)}, u32[]{:S(2)}) collective-permute-start(bf16[4,3,3,64,128]{4,3,2,1,0:T(8,128)(2,1)S(1)} %get-tuple-element.93), channel_id=1, source_target_pairs={{0,3},{1,0},{2,1},{3,2},{4,7},{5,4},{6,5},{7,6},{8,11},{9,8},{10,9... | collective-permute-start | bytes 1769480 | tf_op jit(solution)/shard_map/ppermute | solution.py:374
  128.4 32.2 %collective-permute-start.17 = (bf16[4,3,3,64,128]{4,3,2,1,0:T(8,128)(2,1)S(1)}, bf16[4,3,3,64,128]{4,3,2,1,0:T(8,128)(2,1)S(1)}, u32[]{:S(2)}, u32[]{:S(2)}) collective-permute-start(bf16[4,3,3,64,128]{4,3,2,1,0:T(8,128)(2,1)S(1)} %get-tuple-element.80), channel_id=1, source_target_pairs={{0,8},{1,9},{2,10},{3,11},{4,12},{5,13},{6,14},{7,15},{8,0},{9,1},... | collective-permute-start | bytes 1769480 | tf_op jit(solution)/shard_map/ppermute | solution.py:374
  128.4 32.2 %collective-permute-start.21 = (bf16[4,3,3,64,128]{4,3,2,1,0:T(8,128)(2,1)S(1)}, bf16[4,3,3,64,128]{4,3,2,1,0:T(8,128)(2,1)S(1)}, u32[]{:S(2)}, u32[]{:S(2)}) collective-permute-start(bf16[4,3,3,64,128]{4,3,2,1,0:T(8,128)(2,1)S(1)} %get-tuple-element.85), channel_id=1, source_target_pairs={{0,2},{1,3},{2,0},{3,1},{4,6},{5,7},{6,4},{7,5},{8,10},{9,11},{10,... | collective-permute-start | bytes 1769480 | tf_op jit(solution)/shard_map/ppermute | solution.py:374
  128.5 32.0 %collective-permute-start.25 = (bf16[4,3,1,64,128]{4,3,2,1,0:T(8,128)(2,1)S(1)}, bf16[4,3,1,64,128]{4,3,2,1,0:T(8,128)(2,1)S(1)}, u32[]{:S(2)}, u32[]{:S(2)}) collective-permute-start(bf16[4,3,1,64,128]{4,3,2,1,0:T(8,128)(2,1)S(1)} %get-tuple-element.89), channel_id=1, source_target_pairs={{0,3},{1,0},{2,1},{3,2},{4,7},{5,4},{6,5},{7,6},{8,11},{9,8},{10,9... | collective-permute-start | bytes 589832 | tf_op jit(solution)/shard_map/ppermute | solution.py:374
  152.5 10.0 %collective-permute-start.9 = (bf16[4,3,1,64,128]{4,3,2,1,0:T(8,128)(2,1)S(1)}, bf16[4,3,1,64,128]{4,3,2,1,0:T(8,128)(2,1)S(1)}, u32[]{:S(2)}, u32[]{:S(2)}) collective-permute-start(bf16[4,3,1,64,128]{4,3,2,1,0:T(8,128)(2,1)S(1)} %get-tuple-element.70), channel_id=1, source_target_pairs={{0,8},{1,9},{2,10},{3,11},{4,12},{5,13},{6,14},{7,15},{8,0},{9,1},... | collective-permute-start | bytes 589832 | tf_op jit(solution)/shard_map/ppermute | solution.py:374
  (11 other events, 62.1 us)

commit v4 on v3

--- a/solution.py
+++ b/solution.py
@@ -61,15 +61,17 @@
     lane = lax.broadcasted_iota(jnp.int32, columns.shape, 1)
 
     def expert(e, carry):
-        for i in range(6):
-            fetch(i, e).wait()
         for t in range(2):
+            fetch(2 * t, e).wait()
+            fetch(2 * t + 1, e).wait()
             m, s = held[2 * t], held[2 * t + 1]
             for g in range(groups):
                 part = slice(g * LANES, (g + 1) * LANES)
                 x = m[e, :, part] + s[e, :, part].astype(F32)
                 merged[t][e, :, part] = x
                 out[t * experts + e, g : g + 1, :] = jnp.sum(x * x, axis=0, keepdims=True)
+        fetch(4, e).wait()
+        fetch(5, e).wait()
         so_far = columns[...]
         for g in range(groups):
             part = slice(g * LANES, (g + 1) * LANES)

time: 167 us -> 167 us (level)
  no operation moved by 1% of the time
where the time goes in v4:
time: 167 us; the launch traced here: 164 us
  waiting for transfers between devices  103 us (62%)
  starting transfers between devices  37.8 us (23%)
  Pallas kernels  21.6 us (13%)
    ppermute x12, waiting for transfers between devices, body(): half[k].append(lax.ppermute(send[k, step], 'rows', ways[step][k % 2]))  50.3 us
    ppermute x12, waiting for transfers between devices, body(): whole[step] = lax.ppermute(parts[step], 'rows', ways[step][1 - k % 2])  40.3 us
    ppermute x9, starting transfers between devices, from_all(): came.append(lax.ppermute(a, axis, way))  16 us
    ppermute x9, waiting for transfers between devices, from_all(): came.append(lax.ppermute(a, axis, way))  12.8 us
    ppermute x12, starting transfers between devices, body(): half[k].append(lax.ppermute(send[k, step], 'rows', ways[step][k % 2]))  12.1 us
    ppermute x12, starting transfers between devices, body(): whole[step] = lax.ppermute(parts[step], 'rows', ways[step][1 - k % 2])  9.65 us
    pallas_call x1, Pallas kernels, local_sums(): pl.pallas_call(sums_kernel, in_specs=[ANY] * 8, out_specs=[VMEM] * 4, out...  7.15 us
    pallas_call x4, Pallas kernels, side_by_side(): pl.pallas_call(lambda *refs, picks=picks: place_kernel(picks, *refs), in_...  6.18 us
  transfers between devices with their start and end apart: 34, of which 15 were waited for; matrix products, arithmetic and copies ran while one was open for 0% of the time, Pallas kernels for 6%

profile of v4, /device:TPU:0, one launch (start us, length us, event | category | flops | bytes accessed | tf_op | source)
XLA Modules:
  0.0 163.8 jit_solution(7911115749832024255)
XLA Ops:
  0.6 7.2 %sums.1 = (f32[25,8,128]{2,1,0:T(8,128)S(1)}, f32[8,128,1024]{2,1,0:T(8,128)S(1)}, f32[8,128,1024]{2,1,0:T(8,128)S(1)}, f32[8,1024,128]{2,1,0:T(8,128)S(1)}) custom-call(f32[8,128,1024]{2,1,0:T(8,128)} %refs_0_.3, bf16[8,128,1024]{2,1,0:T(8,128)(2,1)} %refs_1_.1, f32[8,128,1024]{2,1,0:T(8,128)} %refs_2_.1, bf16[8,128,1024]{2,1,0:T(8,128)(2,1)} %refs_3_.1, ...), custom_call_target="tpu_custom_call" | custom-call | flops 9437184 | bytes 18874368 | tf_op jit(solution)/shard_map/sums/pallas_call | solution.py:94
  7.8 3.2 %collective-permute-start.2 = (f32[25,8,128]{2,1,0:T(8,128)S(1)}, f32[25,8,128]{2,1,0:T(8,128)S(1)}, u32[]{:S(2)}, u32[]{:S(2)}) collective-permute-start(f32[25,8,128]{2,1,0:T(8,128)S(1)} %get-tuple-element.61.refs_0_), channel_id=1, source_target_pairs={{0,3},{1,0},{2,1},{3,2},{4,7},{5,4},{6,5},{7,6},{8,11},{9,8},{10,9... | collective-permute-start | bytes 307208 | tf_op jit(solution)/shard_map/ppermute | solution.py:353
  11.0 2.2 %collective-permute-start = (f32[25,8,128]{2,1,0:T(8,128)S(1)}, f32[25,8,128]{2,1,0:T(8,128)S(1)}, u32[]{:S(2)}, u32[]{:S(2)}) collective-permute-start(f32[25,8,128]{2,1,0:T(8,128)S(1)} %get-tuple-element.61.refs_0_), channel_id=1, source_target_pairs={{0,2},{1,3},{2,0},{3,1},{4,6},{5,7},{6,4},{7,5},{8,10},{9,11},{10,... | collective-permute-start | bytes 307208 | tf_op jit(solution)/shard_map/ppermute | solution.py:353
  13.2 5.5 %collective-permute-done.1.refs_2_ = f32[25,8,128]{2,1,0:T(8,128)S(1)} collective-permute-done((f32[25,8,128]{2,1,0:T(8,128)S(1)}, f32[25,8,128]{2,1,0:T(8,128)S(1)}, u32[]{:S(2)}, u32[]{:S(2)}) %collective-permute-start.1) | collective-permute-done | bytes 102432 | tf_op jit(solution)/shard_map/ppermute | solution.py:353
  18.8 4.1 %collective-permute-start.5 = (f32[28,8,128]{2,1,0:T(8,128)S(1)}, f32[28,8,128]{2,1,0:T(8,128)S(1)}, u32[]{:S(2)}, u32[]{:S(2)}) collective-permute-start(f32[28,8,128]{2,1,0:T(8,128)S(1)} %shard_map.144.refs_1_), channel_id=1, source_target_pairs={{0,12},{1,13},{2,14},{3,15},{4,0},{5,1},{6,2},{7,3},{8,4},{9,5},{1... | collective-permute-start | bytes 344072 | tf_op jit(solution)/shard_map/ppermute | solution.py:353
  22.9 1.9 %collective-permute-start.3 = (f32[28,8,128]{2,1,0:T(8,128)S(1)}, f32[28,8,128]{2,1,0:T(8,128)S(1)}, u32[]{:S(2)}, u32[]{:S(2)}) collective-permute-start(f32[28,8,128]{2,1,0:T(8,128)S(1)} %shard_map.144.refs_1_), channel_id=1, source_target_pairs={{0,8},{1,9},{2,10},{3,11},{4,12},{5,13},{6,14},{7,15},{8,0},{9,1},... | collective-permute-start | bytes 344072 | tf_op jit(solution)/shard_map/ppermute | solution.py:353
  28.0 2.1 %collective-permute-done.4.refs_3_ = f32[28,8,128]{2,1,0:T(8,128)S(1)} collective-permute-done((f32[28,8,128]{2,1,0:T(8,128)S(1)}, f32[28,8,128]{2,1,0:T(8,128)S(1)}, u32[]{:S(2)}, u32[]{:S(2)}) %collective-permute-start.4) | collective-permute-done | bytes 114720 | tf_op jit(solution)/shard_map/ppermute | solution.py:353
  31.0 2.2 %scale_2.1 = (bf16[4,3,3,64,128]{4,3,2,1,0:T(8,128)(2,1)S(1)}, bf16[4,3,3,64,128]{4,3,2,1,0:T(8,128)(2,1)S(1)}, bf16[4,3,3,64,128]{4,3,2,1,0:T(8,128)(2,1)S(1)},...) custom-call(bf16[128,3072]{1,0:T(8,128)(2,1)S(1)} %copy-done, ...), custom_call_target="tpu_custom_call" | custom-call | flops 3145728 | bytes 9437184 | tf_op jit(solution)/shard_map/scale_2/pallas_call | solution.py:214
  33.4 3.3 %collective-permute-start.16 = (bf16[4,3,3,64,128]{4,3,2,1,0:T(8,128)(2,1)S(1)}, bf16[4,3,3,64,128]{4,3,2,1,0:T(8,128)(2,1)S(1)}, u32[]{:S(2)}, u32[]{:S(2)}) collective-permute-start(bf16[4,3,3,64,128]{4,3,2,1,0:T(8,128)(2,1)S(1)} %get-tuple-element.79), channel_id=1, source_target_pairs={{0,3},{1,0},{2,1},{3,2},{4,7},{5,4},{6,5},{7,6},{8,11},{9,8},{10,9... | collective-permute-start | bytes 1769480 | tf_op jit(solution)/shard_map/ppermute | solution.py:370
  36.6 2.8 %collective-permute-start.32 = (bf16[8,2048]{1,0:T(8,128)(2,1)S(1)}, bf16[8,2048]{1,0:T(8,128)(2,1)S(1)}, u32[]{:S(2)}, u32[]{:S(2)}) collective-permute-start(bf16[8,2048]{1,0:T(8,128)(2,1)S(1)} %shard_map.155.a), channel_id=1, source_target_pairs={{0,96},{16,112},{32,0},{48,16},{64,32},{80,48},{96,64},{112,80},{1... | collective-permute-start | bytes 98312 | tf_op jit(solution)/shard_map/ppermute | solution.py:353
  42.1 2.8 %collective-permute-done.31.c = bf16[8,2048]{1,0:T(8,128)(2,1)S(1)} collective-permute-done((bf16[8,2048]{1,0:T(8,128)(2,1)S(1)}, bf16[8,2048]{1,0:T(8,128)(2,1)S(1)}, u32[]{:S(2)}, u32[]{:S(2)}) %collective-permute-start.31) | collective-permute-done | bytes 32800 | tf_op jit(solution)/shard_map/ppermute | solution.py:353
  46.5 2.5 %collective-permute-start.6 = (bf16[4,3,1,64,128]{4,3,2,1,0:T(8,128)(2,1)S(1)}, bf16[4,3,1,64,128]{4,3,2,1,0:T(8,128)(2,1)S(1)}, u32[]{:S(2)}, u32[]{:S(2)}) collective-permute-start(bf16[4,3,1,64,128]{4,3,2,1,0:T(8,128)(2,1)S(1)} %get-tuple-element.67), channel_id=1, source_target_pairs={{0,2},{1,3},{2,0},{3,1},{4,6},{5,7},{6,4},{7,5},{8,10},{9,11},{10,... | collective-permute-start | bytes 589832 | tf_op jit(solution)/shard_map/ppermute | solution.py:370
  49.1 16.3 %collective-permute-done.6.refs_1_ = bf16[4,3,1,64,128]{4,3,2,1,0:T(8,128)(2,1)S(1)} collective-permute-done((bf16[4,3,1,64,128]{4,3,2,1,0:T(8,128)(2,1)S(1)}, bf16[4,3,1,64,128]{4,3,2,1,0:T(8,128)(2,1)S(1)}, u32[]{:S(2)}, u32[]{:S(2)}) %collective-permute-start.6) | collective-permute-done | bytes 196640 | tf_op jit(solution)/shard_map/ppermute | solution.py:370
  65.8 1.9 %collective-permute-done.7.refs_2_ = bf16[4,3,1,64,128]{4,3,2,1,0:T(8,128)(2,1)S(1)} collective-permute-done((bf16[4,3,1,64,128]{4,3,2,1,0:T(8,128)(2,1)S(1)}, bf16[4,3,1,64,128]{4,3,2,1,0:T(8,128)(2,1)S(1)}, u32[]{:S(2)}, u32[]{:S(2)}) %collective-permute-start.7) | collective-permute-done | bytes 196640 | tf_op jit(solution)/shard_map/ppermute | solution.py:370
  68.4 2.6 %collective-permute-done.8.refs_3_ = bf16[4,3,1,64,128]{4,3,2,1,0:T(8,128)(2,1)S(1)} collective-permute-done((bf16[4,3,1,64,128]{4,3,2,1,0:T(8,128)(2,1)S(1)}, bf16[4,3,1,64,128]{4,3,2,1,0:T(8,128)(2,1)S(1)}, u32[]{:S(2)}, u32[]{:S(2)}) %collective-permute-start.8) | collective-permute-done | bytes 196640 | tf_op jit(solution)/shard_map/ppermute | solution.py:370
  71.8 2.7 %collective-permute-start.20 = (bf16[4,3,3,64,128]{4,3,2,1,0:T(8,128)(2,1)S(1)}, bf16[4,3,3,64,128]{4,3,2,1,0:T(8,128)(2,1)S(1)}, u32[]{:S(2)}, u32[]{:S(2)}) collective-permute-start(bf16[4,3,3,64,128]{4,3,2,1,0:T(8,128)(2,1)S(1)} %get-tuple-element.84), channel_id=1, source_target_pairs={{0,12},{1,13},{2,14},{3,15},{4,0},{5,1},{6,2},{7,3},{8,4},{9,5},{1... | collective-permute-start | bytes 1769480 | tf_op jit(solution)/shard_map/ppermute | solution.py:370
  76.2 13.4 %collective-permute-done.10.refs_1_ = bf16[4,3,1,64,128]{4,3,2,1,0:T(8,128)(2,1)S(1)} collective-permute-done((bf16[4,3,1,64,128]{4,3,2,1,0:T(8,128)(2,1)S(1)}, bf16[4,3,1,64,128]{4,3,2,1,0:T(8,128)(2,1)S(1)}, u32[]{:S(2)}, u32[]{:S(2)}) %collective-permute-start.10) | collective-permute-done | bytes 196640 | tf_op jit(solution)/shard_map/ppermute | solution.py:370
  89.7 15.4 %collective-permute-done.11.refs_2_ = bf16[4,3,1,64,128]{4,3,2,1,0:T(8,128)(2,1)S(1)} collective-permute-done((bf16[4,3,1,64,128]{4,3,2,1,0:T(8,128)(2,1)S(1)}, bf16[4,3,1,64,128]{4,3,2,1,0:T(8,128)(2,1)S(1)}, u32[]{:S(2)}, u32[]{:S(2)}) %collective-permute-start.11) | collective-permute-done | bytes 196640 | tf_op jit(solution)/shard_map/ppermute | solution.py:370
  106.2 2.8 %collective-permute-start.24 = (bf16[4,3,1,64,128]{4,3,2,1,0:T(8,128)(2,1)S(1)}, bf16[4,3,1,64,128]{4,3,2,1,0:T(8,128)(2,1)S(1)}, u32[]{:S(2)}, u32[]{:S(2)}) collective-permute-start(bf16[4,3,1,64,128]{4,3,2,1,0:T(8,128)(2,1)S(1)} %get-tuple-element.88), channel_id=1, source_target_pairs={{0,12},{1,13},{2,14},{3,15},{4,0},{5,1},{6,2},{7,3},{8,4},{9,5},{1... | collective-permute-start | bytes 589832 | tf_op jit(solution)/shard_map/ppermute | solution.py:376
  110.9 14.0 %collective-permute-done.22.refs_2_ = bf16[4,3,1,64,128]{4,3,2,1,0:T(8,128)(2,1)S(1)} collective-permute-done((bf16[4,3,1,64,128]{4,3,2,1,0:T(8,128)(2,1)S(1)}, bf16[4,3,1,64,128]{4,3,2,1,0:T(8,128)(2,1)S(1)}, u32[]{:S(2)}, u32[]{:S(2)}) %collective-permute-start.22) | collective-permute-done | bytes 196640 | tf_op jit(solution)/shard_map/ppermute | solution.py:376
  124.9 3.2 %collective-permute-start.29 = (bf16[4,3,3,64,128]{4,3,2,1,0:T(8,128)(2,1)S(1)}, bf16[4,3,3,64,128]{4,3,2,1,0:T(8,128)(2,1)S(1)}, u32[]{:S(2)}, u32[]{:S(2)}) collective-permute-start(bf16[4,3,3,64,128]{4,3,2,1,0:T(8,128)(2,1)S(1)} %get-tuple-element.93), channel_id=1, source_target_pairs={{0,3},{1,0},{2,1},{3,2},{4,7},{5,4},{6,5},{7,6},{8,11},{9,8},{10,9... | collective-permute-start | bytes 1769480 | tf_op jit(solution)/shard_map/ppermute | solution.py:376
  129.7 22.6 %collective-permute-done.27.refs_1_ = bf16[4,3,3,64,128]{4,3,2,1,0:T(8,128)(2,1)S(1)} collective-permute-done((bf16[4,3,3,64,128]{4,3,2,1,0:T(8,128)(2,1)S(1)}, bf16[4,3,3,64,128]{4,3,2,1,0:T(8,128)(2,1)S(1)}, u32[]{:S(2)}, u32[]{:S(2)}) %collective-permute-start.27) | collective-permute-done | bytes 589856 | tf_op jit(solution)/shard_map/ppermute | solution.py:376
  152.3 3.2 %collective-permute-done.29.refs_3_ = bf16[4,3,3,64,128]{4,3,2,1,0:T(8,128)(2,1)S(1)} collective-permute-done((bf16[4,3,3,64,128]{4,3,2,1,0:T(8,128)(2,1)S(1)}, bf16[4,3,3,64,128]{4,3,2,1,0:T(8,128)(2,1)S(1)}, u32[]{:S(2)}, u32[]{:S(2)}) %collective-permute-start.29) | collective-permute-done | bytes 589856 | tf_op jit(solution)/shard_map/ppermute | solution.py:376
  160.4 1.9 %shard_map.153 = (bf16[8,64,2048]{2,1,0:T(8,128)(2,1)}, bf16[8,64,2048]{2,1,0:T(8,128)(2,1)}, bf16[8,64,2048]{2,1,0:T(8,128)(2,1)}) custom-call(bf16[4,3,3,64,128]{4,3,2,1,0:T(8,128)(2,1)S(1)} %collective-permute-done.17.refs_0_, ...), custom_call_target="tpu_custom_call", output_to_operand_aliasing={{0}: (6, {}), {1}: (7, {}), {2}: (8, {})} | custom-call | bytes 7077888 | tf_op jit(solution)/shard_map/pallas_call | solution.py:269
  (64 shorter events, 23.0 us)
Async XLA Ops:
  11.0 7.7 %collective-permute-start.1 = (f32[25,8,128]{2,1,0:T(8,128)S(1)}, f32[25,8,128]{2,1,0:T(8,128)S(1)}, u32[]{:S(2)}, u32[]{:S(2)}) collective-permute-start(f32[25,8,128]{2,1,0:T(8,128)S(1)} %get-tuple-element.61.refs_0_), channel_id=1, source_target_pairs={{0,1},{1,2},{2,3},{3,0},{4,5},{5,6},{6,7},{7,4},{8,9},{9,10},{10,1... | collective-permute-start | bytes 307208 | tf_op jit(solution)/shard_map/ppermute | solution.py:353
  18.8 9.3 %collective-permute-start.5 = (f32[28,8,128]{2,1,0:T(8,128)S(1)}, f32[28,8,128]{2,1,0:T(8,128)S(1)}, u32[]{:S(2)}, u32[]{:S(2)}) collective-permute-start(f32[28,8,128]{2,1,0:T(8,128)S(1)} %shard_map.144.refs_1_), channel_id=1, source_target_pairs={{0,12},{1,13},{2,14},{3,15},{4,0},{5,1},{6,2},{7,3},{8,4},{9,5},{1... | collective-permute-start | bytes 344072 | tf_op jit(solution)/shard_map/ppermute | solution.py:353
  33.3 38.5 %collective-permute-start.15 = (bf16[4,3,3,64,128]{4,3,2,1,0:T(8,128)(2,1)S(1)}, bf16[4,3,3,64,128]{4,3,2,1,0:T(8,128)(2,1)S(1)}, u32[]{:S(2)}, u32[]{:S(2)}) collective-permute-start(bf16[4,3,3,64,128]{4,3,2,1,0:T(8,128)(2,1)S(1)} %get-tuple-element.78), channel_id=1, source_target_pairs={{0,1},{1,2},{2,3},{3,0},{4,5},{5,6},{6,7},{7,4},{8,9},{9,10},{10,1... | collective-permute-start | bytes 1769480 | tf_op jit(solution)/shard_map/ppermute | solution.py:370
  33.4 41.1 %collective-permute-start.16 = (bf16[4,3,3,64,128]{4,3,2,1,0:T(8,128)(2,1)S(1)}, bf16[4,3,3,64,128]{4,3,2,1,0:T(8,128)(2,1)S(1)}, u32[]{:S(2)}, u32[]{:S(2)}) collective-permute-start(bf16[4,3,3,64,128]{4,3,2,1,0:T(8,128)(2,1)S(1)} %get-tuple-element.79), channel_id=1, source_target_pairs={{0,3},{1,0},{2,1},{3,2},{4,7},{5,4},{6,5},{7,6},{8,11},{9,8},{10,9... | collective-permute-start | bytes 1769480 | tf_op jit(solution)/shard_map/ppermute | solution.py:370
  39.4 36.7 %collective-permute-start.14 = (bf16[4,3,3,64,128]{4,3,2,1,0:T(8,128)(2,1)S(1)}, bf16[4,3,3,64,128]{4,3,2,1,0:T(8,128)(2,1)S(1)}, u32[]{:S(2)}, u32[]{:S(2)}) collective-permute-start(bf16[4,3,3,64,128]{4,3,2,1,0:T(8,128)(2,1)S(1)} %get-tuple-element.77), channel_id=1, source_target_pairs={{0,2},{1,3},{2,0},{3,1},{4,6},{5,7},{6,4},{7,5},{8,10},{9,11},{10,... | collective-permute-start | bytes 1769480 | tf_op jit(solution)/shard_map/ppermute | solution.py:370
  46.5 18.8 %collective-permute-start.6 = (bf16[4,3,1,64,128]{4,3,2,1,0:T(8,128)(2,1)S(1)}, bf16[4,3,1,64,128]{4,3,2,1,0:T(8,128)(2,1)S(1)}, u32[]{:S(2)}, u32[]{:S(2)}) collective-permute-start(bf16[4,3,1,64,128]{4,3,2,1,0:T(8,128)(2,1)S(1)} %get-tuple-element.67), channel_id=1, source_target_pairs={{0,2},{1,3},{2,0},{3,1},{4,6},{5,7},{6,4},{7,5},{8,10},{9,11},{10,... | collective-permute-start | bytes 589832 | tf_op jit(solution)/shard_map/ppermute | solution.py:370
  49.1 18.6 %collective-permute-start.7 = (bf16[4,3,1,64,128]{4,3,2,1,0:T(8,128)(2,1)S(1)}, bf16[4,3,1,64,128]{4,3,2,1,0:T(8,128)(2,1)S(1)}, u32[]{:S(2)}, u32[]{:S(2)}) collective-permute-start(bf16[4,3,1,64,128]{4,3,2,1,0:T(8,128)(2,1)S(1)} %get-tuple-element.68), channel_id=1, source_target_pairs={{0,1},{1,2},{2,3},{3,0},{4,5},{5,6},{6,7},{7,4},{8,9},{9,10},{10,1... | collective-permute-start | bytes 589832 | tf_op jit(solution)/shard_map/ppermute | solution.py:370
  67.6 38.6 %collective-permute-start.19 = (bf16[4,3,3,64,128]{4,3,2,1,0:T(8,128)(2,1)S(1)}, bf16[4,3,3,64,128]{4,3,2,1,0:T(8,128)(2,1)S(1)}, u32[]{:S(2)}, u32[]{:S(2)}) collective-permute-start(bf16[4,3,3,64,128]{4,3,2,1,0:T(8,128)(2,1)S(1)} %get-tuple-element.83), channel_id=1, source_target_pairs={{0,4},{1,5},{2,6},{3,7},{4,8},{5,9},{6,10},{7,11},{8,12},{9,13},{1... | collective-permute-start | bytes 1769480 | tf_op jit(solution)/shard_map/ppermute | solution.py:370
  71.0 18.7 %collective-permute-start.10 = (bf16[4,3,1,64,128]{4,3,2,1,0:T(8,128)(2,1)S(1)}, bf16[4,3,1,64,128]{4,3,2,1,0:T(8,128)(2,1)S(1)}, u32[]{:S(2)}, u32[]{:S(2)}) collective-permute-start(bf16[4,3,1,64,128]{4,3,2,1,0:T(8,128)(2,1)S(1)} %get-tuple-element.72), channel_id=1, source_target_pairs={{0,8},{1,9},{2,10},{3,11},{4,12},{5,13},{6,14},{7,15},{8,0},{9,1},... | collective-permute-start | bytes 589832 | tf_op jit(solution)/shard_map/ppermute | solution.py:370
  71.8 37.3 %collective-permute-start.20 = (bf16[4,3,3,64,128]{4,3,2,1,0:T(8,128)(2,1)S(1)}, bf16[4,3,3,64,128]{4,3,2,1,0:T(8,128)(2,1)S(1)}, u32[]{:S(2)}, u32[]{:S(2)}) collective-permute-start(bf16[4,3,3,64,128]{4,3,2,1,0:T(8,128)(2,1)S(1)} %get-tuple-element.84), channel_id=1, source_target_pairs={{0,12},{1,13},{2,14},{3,15},{4,0},{5,1},{6,2},{7,3},{8,4},{9,5},{1... | collective-permute-start | bytes 1769480 | tf_op jit(solution)/shard_map/ppermute | solution.py:370
  74.5 34.7 %collective-permute-start.18 = (bf16[4,3,3,64,128]{4,3,2,1,0:T(8,128)(2,1)S(1)}, bf16[4,3,3,64,128]{4,3,2,1,0:T(8,128)(2,1)S(1)}, u32[]{:S(2)}, u32[]{:S(2)}) collective-permute-start(bf16[4,3,3,64,128]{4,3,2,1,0:T(8,128)(2,1)S(1)} %get-tuple-element.82), channel_id=1, source_target_pairs={{0,8},{1,9},{2,10},{3,11},{4,12},{5,13},{6,14},{7,15},{8,0},{9,1},... | collective-permute-start | bytes 1769480 | tf_op jit(solution)/shard_map/ppermute | solution.py:370
  76.1 29.1 %collective-permute-start.11 = (bf16[4,3,1,64,128]{4,3,2,1,0:T(8,128)(2,1)S(1)}, bf16[4,3,1,64,128]{4,3,2,1,0:T(8,128)(2,1)S(1)}, u32[]{:S(2)}, u32[]{:S(2)}) collective-permute-start(bf16[4,3,1,64,128]{4,3,2,1,0:T(8,128)(2,1)S(1)} %get-tuple-element.73), channel_id=1, source_target_pairs={{0,4},{1,5},{2,6},{3,7},{4,8},{5,9},{6,10},{7,11},{8,12},{9,13},{1... | collective-permute-start | bytes 589832 | tf_op jit(solution)/shard_map/ppermute | solution.py:370
  89.7 16.1 %collective-permute-start.12 = (bf16[4,3,1,64,128]{4,3,2,1,0:T(8,128)(2,1)S(1)}, bf16[4,3,1,64,128]{4,3,2,1,0:T(8,128)(2,1)S(1)}, u32[]{:S(2)}, u32[]{:S(2)}) collective-permute-start(bf16[4,3,1,64,128]{4,3,2,1,0:T(8,128)(2,1)S(1)} %get-tuple-element.74), channel_id=1, source_target_pairs={{0,12},{1,13},{2,14},{3,15},{4,0},{5,1},{6,2},{7,3},{8,4},{9,5},{1... | collective-permute-start | bytes 589832 | tf_op jit(solution)/shard_map/ppermute | solution.py:370
  105.1 23.1 %collective-permute-start.26 = (bf16[4,3,3,64,128]{4,3,2,1,0:T(8,128)(2,1)S(1)}, bf16[4,3,3,64,128]{4,3,2,1,0:T(8,128)(2,1)S(1)}, u32[]{:S(2)}, u32[]{:S(2)}) collective-permute-start(bf16[4,3,3,64,128]{4,3,2,1,0:T(8,128)(2,1)S(1)} %get-tuple-element.90), channel_id=1, source_target_pairs={{0,4},{1,5},{2,6},{3,7},{4,8},{5,9},{6,10},{7,11},{8,12},{9,13},{1... | collective-permute-start | bytes 1769480 | tf_op jit(solution)/shard_map/ppermute | solution.py:376
  105.8 19.1 %collective-permute-start.22 = (bf16[4,3,1,64,128]{4,3,2,1,0:T(8,128)(2,1)S(1)}, bf16[4,3,1,64,128]{4,3,2,1,0:T(8,128)(2,1)S(1)}, u32[]{:S(2)}, u32[]{:S(2)}) collective-permute-start(bf16[4,3,1,64,128]{4,3,2,1,0:T(8,128)(2,1)S(1)} %get-tuple-element.86), channel_id=1, source_target_pairs={{0,4},{1,5},{2,6},{3,7},{4,8},{5,9},{6,10},{7,11},{8,12},{9,13},{1... | collective-permute-start | bytes 589832 | tf_op jit(solution)/shard_map/ppermute | solution.py:376
  106.2 18.7 %collective-permute-start.24 = (bf16[4,3,1,64,128]{4,3,2,1,0:T(8,128)(2,1)S(1)}, bf16[4,3,1,64,128]{4,3,2,1,0:T(8,128)(2,1)S(1)}, u32[]{:S(2)}, u32[]{:S(2)}) collective-permute-start(bf16[4,3,1,64,128]{4,3,2,1,0:T(8,128)(2,1)S(1)} %get-tuple-element.88), channel_id=1, source_target_pairs={{0,12},{1,13},{2,14},{3,15},{4,0},{5,1},{6,2},{7,3},{8,4},{9,5},{1... | collective-permute-start | bytes 589832 | tf_op jit(solution)/shard_map/ppermute | solution.py:376
  109.1 19.1 %collective-permute-start.23 = (bf16[4,3,1,64,128]{4,3,2,1,0:T(8,128)(2,1)S(1)}, bf16[4,3,1,64,128]{4,3,2,1,0:T(8,128)(2,1)S(1)}, u32[]{:S(2)}, u32[]{:S(2)}) collective-permute-start(bf16[4,3,1,64,128]{4,3,2,1,0:T(8,128)(2,1)S(1)} %get-tuple-element.87), channel_id=1, source_target_pairs={{0,1},{1,2},{2,3},{3,0},{4,5},{5,6},{6,7},{7,4},{8,9},{9,10},{10,1... | collective-permute-start | bytes 589832 | tf_op jit(solution)/shard_map/ppermute | solution.py:376
  109.2 19.1 %collective-permute-start.28 = (bf16[4,3,3,64,128]{4,3,2,1,0:T(8,128)(2,1)S(1)}, bf16[4,3,3,64,128]{4,3,2,1,0:T(8,128)(2,1)S(1)}, u32[]{:S(2)}, u32[]{:S(2)}) collective-permute-start(bf16[4,3,3,64,128]{4,3,2,1,0:T(8,128)(2,1)S(1)} %get-tuple-element.92), channel_id=1, source_target_pairs={{0,12},{1,13},{2,14},{3,15},{4,0},{5,1},{6,2},{7,3},{8,4},{9,5},{1... | collective-permute-start | bytes 1769480 | tf_op jit(solution)/shard_map/ppermute | solution.py:376
  124.9 27.4 %collective-permute-start.27 = (bf16[4,3,3,64,128]{4,3,2,1,0:T(8,128)(2,1)S(1)}, bf16[4,3,3,64,128]{4,3,2,1,0:T(8,128)(2,1)S(1)}, u32[]{:S(2)}, u32[]{:S(2)}) collective-permute-start(bf16[4,3,3,64,128]{4,3,2,1,0:T(8,128)(2,1)S(1)} %get-tuple-element.91), channel_id=1, source_target_pairs={{0,1},{1,2},{2,3},{3,0},{4,5},{5,6},{6,7},{7,4},{8,9},{9,10},{10,1... | collective-permute-start | bytes 1769480 | tf_op jit(solution)/shard_map/ppermute | solution.py:376
  124.9 30.6 %collective-permute-start.29 = (bf16[4,3,3,64,128]{4,3,2,1,0:T(8,128)(2,1)S(1)}, bf16[4,3,3,64,128]{4,3,2,1,0:T(8,128)(2,1)S(1)}, u32[]{:S(2)}, u32[]{:S(2)}) collective-permute-start(bf16[4,3,3,64,128]{4,3,2,1,0:T(8,128)(2,1)S(1)} %get-tuple-element.93), channel_id=1, source_target_pairs={{0,3},{1,0},{2,1},{3,2},{4,7},{5,4},{6,5},{7,6},{8,11},{9,8},{10,9... | collective-permute-start | bytes 1769480 | tf_op jit(solution)/shard_map/ppermute | solution.py:376
  128.2 32.2 %collective-permute-start.17 = (bf16[4,3,3,64,128]{4,3,2,1,0:T(8,128)(2,1)S(1)}, bf16[4,3,3,64,128]{4,3,2,1,0:T(8,128)(2,1)S(1)}, u32[]{:S(2)}, u32[]{:S(2)}) collective-permute-start(bf16[4,3,3,64,128]{4,3,2,1,0:T(8,128)(2,1)S(1)} %get-tuple-element.80), channel_id=1, source_target_pairs={{0,8},{1,9},{2,10},{3,11},{4,12},{5,13},{6,14},{7,15},{8,0},{9,1},... | collective-permute-start | bytes 1769480 | tf_op jit(solution)/shard_map/ppermute | solution.py:376
  128.2 32.2 %collective-permute-start.21 = (bf16[4,3,3,64,128]{4,3,2,1,0:T(8,128)(2,1)S(1)}, bf16[4,3,3,64,128]{4,3,2,1,0:T(8,128)(2,1)S(1)}, u32[]{:S(2)}, u32[]{:S(2)}) collective-permute-start(bf16[4,3,3,64,128]{4,3,2,1,0:T(8,128)(2,1)S(1)} %get-tuple-element.85), channel_id=1, source_target_pairs={{0,2},{1,3},{2,0},{3,1},{4,6},{5,7},{6,4},{7,5},{8,10},{9,11},{10,... | collective-permute-start | bytes 1769480 | tf_op jit(solution)/shard_map/ppermute | solution.py:376
  128.3 32.0 %collective-permute-start.25 = (bf16[4,3,1,64,128]{4,3,2,1,0:T(8,128)(2,1)S(1)}, bf16[4,3,1,64,128]{4,3,2,1,0:T(8,128)(2,1)S(1)}, u32[]{:S(2)}, u32[]{:S(2)}) collective-permute-start(bf16[4,3,1,64,128]{4,3,2,1,0:T(8,128)(2,1)S(1)} %get-tuple-element.89), channel_id=1, source_target_pairs={{0,3},{1,0},{2,1},{3,2},{4,7},{5,4},{6,5},{7,6},{8,11},{9,8},{10,9... | collective-permute-start | bytes 589832 | tf_op jit(solution)/shard_map/ppermute | solution.py:376
  152.3 10.0 %collective-permute-start.9 = (bf16[4,3,1,64,128]{4,3,2,1,0:T(8,128)(2,1)S(1)}, bf16[4,3,1,64,128]{4,3,2,1,0:T(8,128)(2,1)S(1)}, u32[]{:S(2)}, u32[]{:S(2)}) collective-permute-start(bf16[4,3,1,64,128]{4,3,2,1,0:T(8,128)(2,1)S(1)} %get-tuple-element.70), channel_id=1, source_target_pairs={{0,8},{1,9},{2,10},{3,11},{4,12},{5,13},{6,14},{7,15},{8,0},{9,1},... | collective-permute-start | bytes 589832 | tf_op jit(solution)/shard_map/ppermute | solution.py:376
  (11 other events, 62.1 us)
